TPU v7x, 128 devices: a whole 4x4x4 slice. The times are simulated.
128 devices in a mesh: dp: 8 (over y, x_lo), tensor: 16 (over x_hi, z, core).
Axes of the slice: x: 4 (x_hi: 2, x_lo: 2; x = x_hi * 2 + x_lo), y: 4, z: 4, core: 2. Of those that a mesh axis runs over, the one named last changes fastest.
Arguments:
- grad_out: bfloat16 [8192, 8192], P(('dp', 'tensor')), may hold values from -24 to 24
- out_weight: bfloat16 [8192, 8192], P('dp', 'tensor'), may hold values from -0.0625 to 0.0625
- query: bfloat16 [8192, 8192], P('dp', 'tensor'), may hold values from -6 to 6, as said below
- keys: bfloat16 [8192, 512], P('dp'), may hold values from -6 to 6
- values: bfloat16 [8192, 512], P('dp'), may hold values from -6 to 6
- attended: bfloat16 [8192, 8192], P('dp', 'tensor'), may hold values from -6 to 6, as said below
- stats: float32 [64, 8192], P('tensor', 'dp'), as said below
Outputs:
- query_grad: bfloat16 [8192, 8192], P('dp', 'tensor')
- key_grad: bfloat16 [8192, 512], P('dp', 'tensor')
- value_grad: bfloat16 [8192, 512], P('dp', 'tensor')
- weight_grad: bfloat16 [8192, 8192], P('dp', 'tensor')
Inputs may be any that keep to these rules, and one draw needn't show every extreme that they name: query, keys and values are independent draws. attended is the causal attention output of the given query, keys and values within each sequence of 1024 rows: query head h uses key head h // 16, scores scaled by 128 ** -0.5, softmax over keys at or before the query. stats[h, t] is the logarithm of the sum of exp(score) over the keys that row t of head h attends to, for the same scores.
All inputs are finite; a program needn't handle non-finite values.
Results may differ from a plain program's by a relative error of at most 0.013.
Values may be sent and summed in bfloat16 or wider, within the bound.
A program may use at most 192 MiB of HBM per device.

v0:
```python
import jax
import jax.numpy as jnp
from jax import lax
from jax.sharding import Mesh
from jax.sharding import PartitionSpec as P

HD = 128
HEAD_DEV = 4
GROUP = 16
DP = ("dp_0", "dp_1")
DP_TENSOR = ("dp_0", "dp_1", "tensor")


def gathered_by_axis(x, axes, dim):
    if not axes:
        return x
    nearer = lax.all_gather(x, axes[-1], axis=dim, tiled=True)
    return gathered_by_axis(nearer, axes[:-1], dim)


def sum_by_axis(terms, axes):
    subtotal = terms.astype(jnp.bfloat16)
    for axis in axes:
        subtotal = lax.psum_scatter(subtotal, axis, scatter_dimension=0, tiled=True)
    return subtotal.astype(jnp.float32)


def partner(value, axis, apart):
    mask = 2**apart
    pairs = [(source, source ^ mask) for source in range(lax.axis_size(axis))]
    return lax.ppermute(value, axis, pairs)


def attention_grads(query, key_one, value_one, attended, grad_att, stats):
    length = query.shape[0]
    score_scale = HD ** (-0.5)
    query_heads = query.reshape(length, HEAD_DEV, HD)
    grad_heads = grad_att.reshape(length, HEAD_DEV, HD)
    attended_heads = attended.reshape(length, HEAD_DEV, HD)
    positions = jnp.arange(length, dtype=jnp.int32)
    causal = positions[:, None] >= positions[None, :]
    scores = (
        jnp.einsum("qgd,kd->gqk", query_heads, key_one, preferred_element_type=jnp.float32)
        * score_scale
    )
    attention = jnp.where(causal[None], jnp.exp(scores - stats[:, :, None]), 0.0)
    attention_low = attention.astype(jnp.bfloat16)
    grad_attention = jnp.einsum(
        "qgd,kd->gqk", grad_heads, value_one, preferred_element_type=jnp.float32
    )
    row_offset = jnp.sum(
        grad_heads.astype(jnp.float32) * attended_heads.astype(jnp.float32), axis=2
    )
    grad_scores = (attention * (grad_attention - row_offset.T[:, :, None])).astype(jnp.bfloat16)
    query_grad = (
        jnp.einsum("gqk,kd->qgd", grad_scores, key_one, preferred_element_type=jnp.float32)
        * score_scale
    )
    query_grad = query_grad.astype(jnp.bfloat16).reshape(length, HEAD_DEV * HD)
    key_part = (
        jnp.einsum("gqk,qgd->kd", grad_scores, query_heads, preferred_element_type=jnp.float32)
        * score_scale
    )
    value_part = jnp.einsum(
        "gqk,qgd->kd", attention_low, grad_heads, preferred_element_type=jnp.float32
    )
    return (query_grad, key_part, value_part)


def per_device(grad_out, out_weight, query, keys, values, attended, stats):
    grad_rows = lax.all_gather(grad_out, "tensor", axis=0, tiled=True)
    grad_block = grad_rows
    grad_att = jnp.dot(
        grad_block, gathered_by_axis(out_weight, DP, 0), preferred_element_type=jnp.float32
    ).astype(jnp.bfloat16)
    grad_block = grad_rows
    weight_grad = sum_by_axis(
        lax.dot_general(
            grad_block, attended, (((0,), (0,)), ((), ())), preferred_element_type=jnp.float32
        ),
        DP,
    ).astype(jnp.bfloat16)
    tensor_index = lax.axis_index("tensor")
    key_head = tensor_index * HEAD_DEV // GROUP
    key_one = lax.dynamic_slice_in_dim(keys, key_head * HD, HD, 1)
    value_one = lax.dynamic_slice_in_dim(values, key_head * HD, HD, 1)
    query_grad, key_part, value_part = attention_grads(
        query, key_one, value_one, attended, grad_att, stats
    )
    group_span = GROUP // HEAD_DEV
    group_place = tensor_index % group_span
    bit_count = group_span.bit_length() - 1
    running_kv = jnp.stack([key_part, value_part])
    for bit_number in reversed(range(bit_count)):
        half_cols = running_kv.shape[2] // 2
        lower_cols = running_kv[:, :, :half_cols]
        upper_cols = running_kv[:, :, half_cols:]
        upper_half = group_place // (1 << bit_number) % 2 == 1
        kept_cols = jnp.where(upper_half, upper_cols, lower_cols)
        sent_cols = jnp.where(upper_half, lower_cols, upper_cols)
        running_kv = kept_cols + partner(
            sent_cols.astype(jnp.bfloat16), "tensor", bit_number
        ).astype(sent_cols.dtype)
    key_grad = running_kv[0].astype(jnp.bfloat16)
    value_grad = running_kv[1].astype(jnp.bfloat16)
    return (query_grad, key_grad, value_grad, weight_grad)


def solution(mesh):
    torus = Mesh(mesh.devices.reshape(4, 2, mesh.shape["tensor"]), ("dp_0", "dp_1", "tensor"))
    in_specs = (
        P(DP_TENSOR, None),
        P(DP, "tensor"),
        P(DP, "tensor"),
        P(DP, None),
        P(DP, None),
        P(DP, "tensor"),
        P("tensor", DP),
    )
    out_specs = (P(DP, "tensor"), P(DP, "tensor"), P(DP, "tensor"), P(DP, "tensor"))
    return jax.shard_map(
        per_device, mesh=torus, in_specs=in_specs, out_specs=out_specs, check_vma=False
    )
```

profile of v0, /device:TPU:1, one launch (start us, length us, event | category | flops | bytes accessed | tf_op | source)
XLA Modules:
  0.0 373.3 jit_solution(7424440204434012823)
XLA Ops:
  7.2 0.0 copy-start
  7.2 0.0 all-gather.6.cloned.1.call-start
  7.2 0.7 all-gather.6.cloned.1.call-update
  7.9 0.0 all-gather.4.cloned.1.call-start
  8.0 0.7 all-gather.4.cloned.1.call-update
  8.7 0.0 all-gather.8.cloned.1.call-start
  8.7 39.6 %all-gather.6.cloned.1.call-done = bf16[2048,512]{1,0:T(8,128)(2,1)} async-done(((bf16[1024,512]{1,0:T(8,128)(2,1)}), bf16[2048,512]{1,0:T(8,128)(2,1)}) %all-gather.6.cloned.1.call-update) | async-done | bytes 2097168 | tf_op jit(solution)/shard_map/all_gather | solution.py:17
  48.3 0.0 all-gather.8.cloned.1.call-update
  48.3 0.0 copy-start.1
  48.3 0.0 copy-start.2
  48.4 0.0 reduce-scatter.3.cloned.1.call-start
  48.4 112.8 %all-gather.4.cloned.1.call-done = bf16[1024,8192]{1,0:T(8,128)(2,1)} async-done(((bf16[64,8192]{1,0:T(8,128)(2,1)}), bf16[1024,8192]{1,0:T(8,128)(2,1)}) %all-gather.4.cloned.1.call-update) | async-done | bytes 16777232 | tf_op jit(solution)/shard_map/all_gather | solution.py:71
  161.2 14.8 %convolution_convert_fusion = bf16[8192,512]{1,0:T(8,128)(2,1)} fusion(bf16[1024,8192]{1,0:T(8,128)(2,1)} %all-gather.4.cloned.1.call-done, bf16[1024,512]{1,0:T(8,128)(2,1)} %param.12), kind=kOutput, calls=%fused_computation.7 | convolution fusion | flops 8594128896 | bytes 26214400 | tf_op jit(solution)/shard_map/dot_general | solution.py:78
  176.0 0.0 reduce-scatter.3.cloned.1.call-update
  176.0 0.2 reduce-scatter.5.cloned.1.call-start
  176.3 0.0 copy-done.1
  176.3 1.6 copy.26
  177.9 0.0 copy-done.2
  177.9 0.5 copy.27
  178.4 0.3 iota_compare_fusion
  178.7 0.0 copy-start.3
  178.8 0.0 copy-done
  178.8 8.1 %fusion.15 = f32[1024,1024,4]{1,0,2:T(8,128)} fusion(bf16[1024,4,128]{0,2,1:T(8,128)(2,1)S(1)} %bitcast.65, bf16[1024,512]{1,0:T(8,128)(2,1)S(1)} %copy-done, s32[]{:T(128)S(6)} %select_n.56), kind=kOutput, calls=%fused_computation.25 | convolution fusion | flops 1073741824 | bytes 18087940 | tf_op jit(solution)/shard_map/qgd,kd->gqk/dot_general | solution.py:43
  186.9 56.2 %all-gather.8.cloned.1.call-done = bf16[8192,512]{1,0:T(8,128)(2,1)} async-done(((bf16[2048,512]{1,0:T(8,128)(2,1)}), bf16[8192,512]{1,0:T(8,128)(2,1)}) %all-gather.8.cloned.1.call-update) | async-done | bytes 8388624 | tf_op jit(solution)/shard_map/all_gather | solution.py:17
  243.0 15.6 %multiply_reduce_fusion = (f32[1024,4]{0,1:T(4,128)S(1)}, bf16[1024,512]{0,1:T(8,128)(2,1)}) fusion(f32[1024,512]{0,1:T(8,128)} %copy.26, bf16[1024,8192]{1,0:T(8,128)(2,1)} %all-gather.4.cloned.1.call-done, bf16[8192,512]{1,0:T(8,128)(2,1)} %all-gather.8.cloned.1.call-done), kind=kOutput, calls=%fused_computation.12 | convolution fusion | flops 8592027648 | bytes 28327936 | tf_op jit(solution)/shard_map/dot_general | solution.py:73
  258.6 68.3 %reduce-scatter.3.cloned.1.call-done = bf16[2048,512]{1,0:T(8,128)(2,1)} async-done(((bf16[8192,512]{1,0:T(8,128)(2,1)}), bf16[2048,512]{1,0:T(8,128)(2,1)}) %reduce-scatter.3.cloned.1.call-update) | async-done | bytes 2097168 | tf_op jit(solution)/shard_map/reduce_scatter | solution.py:24
  326.9 0.0 reduce-scatter.5.cloned.1.call-update
  327.0 0.0 copy-done.3
  327.0 0.0 copy-done.4
  327.0 0.0 slice-start
  327.0 0.0 slice-start.1
  327.0 0.0 slice-start.2
  327.0 0.0 copy-start.5
  327.0 11.5 %fusion.1 = bf16[4,1024,1024]{1,2,0:T(8,128)(2,1)} fusion(f32[1024,1024,4]{1,0,2:T(8,128)} %fusion.15, bf16[1024,4,128]{0,2,1:T(8,128)(2,1)} %bitcast.67, f32[4,1024]{1,0:T(4,128)S(1)} %bitcast.69, f32[4,1024]{1,0:T(4,128)S(1)} %copy-done.4, pred[1024,1024]{0,1:T(8,128)(4,1)S(1)} %iota_compare_fusion, bf16[1024,512]{1,0:T(8,128)(2,1)} %param.11, ...), kind=kOutput, calls=%fused_computation.2 | convolution fusion | flops 1098907648 | bytes 27557892 | tf_op jit(solution)/shard_map/qgd,kd->gqk/dot_general | solution.py:48
  338.5 7.2 %fusion.9 = f32[1,1024,128]{1,2,0:T(8,128)S(1)} fusion(bf16[4,1024,1024]{1,2,0:T(8,128)(2,1)} %fusion.1, bf16[1024,4,128]{0,2,1:T(8,128)(2,1)S(1)} %bitcast.66), kind=kOutput, calls=%fused_computation.16 | convolution fusion | flops 1073872896 | bytes 9961472 | tf_op jit(solution)/shard_map/gqk,qgd->kd/dot_general | solution.py:61
  345.7 0.0 slice-done
  345.7 0.0 slice-done.1
  345.7 0.0 slice-done.2
  345.7 5.2 %fusion.10 = f32[1,1024,128]{1,2,0:T(8,128)S(1)} fusion(bf16[1024,4,128]{0,2,1:T(8,128)(2,1)S(1)} %bitcast.68, f32[1024,1024,4]{1,0,2:T(8,128)S(1)} %bitcast.63, f32[4,1024]{1,0:T(4,128)S(1)} %copy-done.4, pred[1024,1024]{0,1:T(8,128)(4,1)} %copy-done.3), kind=kOutput, calls=%fused_computation.17 | convolution fusion | flops 1090519040 | bytes 19415040 | tf_op jit(solution)/shard_map/gqk,qgd->kd/dot_general | solution.py:64
  351.0 0.1 select_convert_fusion
  351.0 1.5 collective-permute-start
  352.5 6.0 %collective-permute-done = bf16[2,1024,64]{1,2,0:T(8,128)(2,1)S(1)} collective-permute-done((bf16[2,1024,64]{1,2,0:T(8,128)(2,1)S(1)}, bf16[2,1024,64]{1,2,0:T(8,128)(2,1)S(1)}, u32[]{:S(2)}, u32[]{:S(2)}) %collective-permute-start) | collective-permute-done | bytes 262176 | tf_op jit(solution)/shard_map/ppermute | solution.py:31
  358.4 0.1 convert_add_fusion
  358.6 1.5 collective-permute-start.1
  360.0 4.7 %multiply_convert_fusion = bf16[128,4,1024]{2,0,1:T(8,128)(2,1)S(1)} fusion(bf16[4,1024,1024]{1,2,0:T(8,128)(2,1)} %fusion.1, bf16[1024,512]{1,0:T(8,128)(2,1)S(1)} %copy-done, s32[]{:T(128)S(6)} %select_n.56), kind=kOutput, calls=%fused_computation.11 | convolution fusion | flops 1074790400 | bytes 9699332 | tf_op jit(solution)/shard_map/gqk,kd->qgd/dot_general | solution.py:56
  364.7 1.3 copy.19
  366.1 0.0 collective-permute-done.1
  366.1 0.7 slice_bitcast_fusion
  (8 shorter events, 0.1 us)
Async XLA Ops:
  7.2 171.6 %copy-start = (bf16[1024,512]{1,0:T(8,128)(2,1)S(1)}, bf16[1024,512]{1,0:T(8,128)(2,1)}, u32[]{:S(2)}) copy-start(bf16[1024,512]{1,0:T(8,128)(2,1)} %param.10) | copy-start | bytes 3145732
  7.2 41.1 %all-gather.6.cloned.1.call-start = ((), (), s32[]{:S(2)}) async-start(), calls=%async_computation.3 | async-start | bytes 3145728 | tf_op jit(solution)/shard_map/all_gather | solution.py:17
  7.9 153.3 %all-gather.4.cloned.1.call-start = ((), (), s32[]{:S(2)}) async-start(), calls=%async_computation.2 | async-start | bytes 17825792 | tf_op jit(solution)/shard_map/all_gather | solution.py:71
  8.7 234.3 %all-gather.8.cloned.1.call-start = ((), (), s32[]{:S(2)}) async-start(), calls=%async_computation.4 | async-start | bytes 10485760 | tf_op jit(solution)/shard_map/all_gather | solution.py:17
  48.3 127.9 %copy-start.1 = (bf16[1024,512]{1,0:T(8,128)(2,1)S(1)}, bf16[1024,512]{1,0:T(8,128)(2,1)}, u32[]{:S(2)}) copy-start(bf16[1024,512]{1,0:T(8,128)(2,1)} %param.12) | copy-start | bytes 3145732
  48.3 129.5 %copy-start.2 = (bf16[1024,512]{1,0:T(8,128)(2,1)S(1)}, bf16[1024,512]{1,0:T(8,128)(2,1)}, u32[]{:S(2)}) copy-start(bf16[1024,512]{1,0:T(8,128)(2,1)} %param.9) | copy-start | bytes 3145732
  48.4 278.6 %reduce-scatter.3.cloned.1.call-start = ((), (), s32[]{:S(2)}) async-start(), calls=%async_computation.5 | async-start | bytes 10485760 | tf_op jit(solution)/shard_map/reduce_scatter | solution.py:24
  176.0 190.8 %reduce-scatter.5.cloned.1.call-start = ((), (), s32[]{:S(2)}) async-start(), calls=%async_computation.6 | async-start | bytes 3145728 | tf_op jit(solution)/shard_map/reduce_scatter | solution.py:24
  178.7 148.2 %copy-start.3 = (pred[1024,1024]{0,1:T(8,128)(4,1)}, pred[1024,1024]{0,1:T(8,128)(4,1)S(1)}, u32[]{:S(2)}) copy-start(pred[1024,1024]{0,1:T(8,128)(4,1)S(1)} %iota_compare_fusion) | copy-start | bytes 3145732
  186.9 140.1 %copy-start.4 = (f32[4,1024]{1,0:T(4,128)S(1)}, f32[4,1024]{1,0:T(4,128)}, u32[]{:S(2)}) copy-start(f32[4,1024]{1,0:T(4,128)} %param.13) | copy-start | bytes 49156
  327.0 18.7 %slice-start = ((s8[16777216]{0:T(1024)(128)(4,1)}), s8[4194304]{0:T(1024)(128)(4,1)S(1)}, s32[]{:S(2)}) async-start(s8[16777216]{0:T(1024)(128)(4,1)} %bitcast.62), calls=%async_computation.7 | async-start | bytes 8388608
  327.0 18.7 %slice-start.1 = ((s8[16777216]{0:T(1024)(128)(4,1)}), s8[4194304]{0:T(1024)(128)(4,1)S(1)}, s32[]{:S(2)}) async-start(s8[16777216]{0:T(1024)(128)(4,1)} %bitcast.62), calls=%async_computation.8 | async-start | bytes 8388608
  327.0 18.7 %slice-start.2 = ((s8[16777216]{0:T(1024)(128)(4,1)}), s8[4194304]{0:T(1024)(128)(4,1)S(1)}, s32[]{:S(2)}) async-start(s8[16777216]{0:T(1024)(128)(4,1)} %bitcast.62), calls=%async_computation.9 | async-start | bytes 8388608
  327.0 18.7 %copy-start.5 = (bf16[1024,512]{0,1:T(8,128)(2,1)S(1)}, bf16[1024,512]{0,1:T(8,128)(2,1)}, u32[]{:S(2)}) copy-start(bf16[1024,512]{0,1:T(8,128)(2,1)} %get-tuple-element.11) | copy-start | bytes 3145732
  338.5 7.2 %slice-start.3 = ((s8[16777216]{0:T(1024)(128)(4,1)}), s8[4194304]{0:T(1024)(128)(4,1)S(1)}, s32[]{:S(2)}) async-start(s8[16777216]{0:T(1024)(128)(4,1)} %bitcast.62), calls=%async_computation.10 | async-start | bytes 8388608
  351.0 7.4 %collective-permute-start = (bf16[2,1024,64]{1,2,0:T(8,128)(2,1)S(1)}, bf16[2,1024,64]{1,2,0:T(8,128)(2,1)S(1)}, u32[]{:S(2)}, u32[]{:S(2)}) collective-permute-start(bf16[2,1024,64]{1,2,0:T(8,128)(2,1)S(1)} %select_convert_fusion), channel_id=1, source_target_pairs={{0,2},{1,3},{2,0},{3,1},{4,6},{5,7},{6,4},{7,5},{8,10},{9,11},{10,... | collective-permute-start | bytes 786440 | tf_op jit(solution)/shard_map/ppermute | solution.py:31
  358.6 7.5 %collective-permute-start.1 = (bf16[2,1024,32]{1,2,0:T(8,128)(2,1)S(1)}, bf16[2,1024,32]{1,2,0:T(8,128)(2,1)S(1)}, u32[]{:S(2)}, u32[]{:S(2)}) collective-permute-start(bf16[2,1024,32]{1,2,0:T(8,128)(2,1)S(1)} %select_convert_fusion.1), channel_id=1, source_target_pairs={{0,1},{1,0},{2,3},{3,2},{4,5},{5,4},{6,7},{7,6},{8,9},{9,8},{10,11... | collective-permute-start | bytes 393224 | tf_op jit(solution)/shard_map/ppermute | solution.py:31
Sparse Core Ops, SparseCore 0:
  9.6 38.6 all-gather.5
  50.8 110.3 all-gather.3
  162.9 80.0 all-gather.7
  245.3 81.5 reduce-scatter.2
  329.7 34.0 reduce-scatter.4
where the time goes:
time: 373 us
  waiting for transfers between devices  284 us (76%)
  matrix products  67 us (18%)
  between operations  14 us (4%)
  local copies, waits for them, and re-layouts  4.17 us (1%)
    all_gather x1, waiting for transfers between devices, per_device(): grad_rows = lax.all_gather(grad_out, 'tensor', axis=0, tiled=True)  113 us
    all_gather x2, waiting for transfers between devices, gathered_by_axis(): nearer = lax.all_gather(x, axes[-1], axis=dim, tiled=True)  95.7 us
    reduce_scatter x2, waiting for transfers between devices, sum_by_axis(): subtotal = lax.psum_scatter(subtotal, axis, scatter_dimension=0, tiled=True)  68.3 us
    dot_general x1, matrix products, per_device(): jnp.dot(grad_block, gathered_by_axis(out_weight, DP, 0), preferred_elemen...  15.6 us
    dot_general x1, matrix products, per_device(): lax.dot_general(grad_block, attended, (((0,), (0,)), ((), ())), preferred...  14.8 us
    dot_general x1, matrix products, attention_grads(): jnp.einsum('qgd,kd->gqk', grad_heads, value_one, preferred_element_type=j...  11.5 us
    dot_general x1, matrix products, attention_grads(): jnp.einsum('qgd,kd->gqk', query_heads, key_one, preferred_element_type=jn...  8.09 us
  transfers between devices with their start and end apart: 7, of which 5 were waited for; matrix products, arithmetic and copies ran while one was open for 19% of the time, Pallas kernels for 0%

commit v1 on v0

v1 whole, which is shorter than its diff:
```python
import jax
import jax.numpy as jnp
from jax import lax
from jax.experimental import pallas as pl
from jax.experimental.pallas import tpu as pltpu
from jax.sharding import Mesh
from jax.sharding import PartitionSpec as P

HD = 128
GROUP = 16
BF = jnp.bfloat16
F32 = jnp.float32
AXES = ("y", "xlo", "xhi", "z", "core")
NN = (((1,), (0,)), ((), ()))
NT = (((1,), (1,)), ((), ()))


def dot(a, b, dims=NN):
    return lax.dot_general(a, b, dims, preferred_element_type=F32)


def rcopy(src, dst, send, recv, dev):
    return pltpu.make_async_remote_copy(
        src_ref=src,
        dst_ref=dst,
        send_sem=send,
        recv_sem=recv,
        device_id=dev,
        device_id_type=pl.DeviceIdType.MESH,
    )


def kernel(
    g_in, w_in, q_in, k_in, v_in, a_in, st_in,
    dq_out, kv_out, wg_out,
    G, W, S, RX, RH, RP, RY, AT, ACC, Q, GA, GAT, K, V, KT, A, ST,
    DK, DV, KF, KB, KR1, KB2, KR2,
    xs, xr, us, ur, zs, zr, cs, cr, ws, wr, rs, rr, ks, kr, ls, lq,
):
    y, xlo, xhi = lax.axis_index("y"), lax.axis_index("xlo"), lax.axis_index("xhi")
    z, c = lax.axis_index("z"), lax.axis_index("core")
    scale = HD ** (-0.5)
    yp, ym, y2 = lax.rem(y + 1, 4), lax.rem(y + 3, 4), lax.rem(y + 2, 4)
    zp, zm, z2 = lax.rem(z + 1, 4), lax.rem(z + 3, 4), lax.rem(z + 2, 4)
    xo, xh, co = 1 - xlo, 1 - xhi, 1 - c
    zpair = z + 1 - 2 * lax.rem(z, 2)

    head = xhi * 2 + z // 2
    hcol = pl.ds(pl.multiple_of(head * HD, HD), HD)
    order = ((y2, xo), (y2, xlo), (yp, xo), (ym, xo), (yp, xlo), (ym, xlo), (y, xo), (y, xlo))

    own = []
    for j, (yj, xj) in enumerate(order):
        col = pl.multiple_of((yj * 2 + xj) * 1024, 1024)
        own.append(pltpu.make_async_copy(g_in.at[:, pl.ds(col, 1024)], G.at[j, xhi, z, c], ls.at[j]))
    for cp in own:
        cp.start()
    wcp = pltpu.make_async_copy(w_in, W.at[0], lq.at[0])
    wcp.start()
    acp = pltpu.make_async_copy(a_in, A, lq.at[1])
    acp.start()
    others = [
        pltpu.make_async_copy(k_in.at[:, hcol], K, lq.at[2]),
        pltpu.make_async_copy(v_in.at[:, hcol], V, lq.at[3]),
        pltpu.make_async_copy(st_in, ST, lq.at[4]),
    ]
    for h in range(4):
        others.append(
            pltpu.make_async_copy(q_in.at[:, h * HD : (h + 1) * HD], Q.at[h], lq.at[5 + h])
        )
    for cp in others:
        cp.start()

    barrier = pltpu.get_barrier_semaphore()
    for dev in ({"y": yp}, {"y": ym}, {"xlo": xo}, {"xhi": xh}, {"z": zp}, {"z": zm}, {"core": co}):
        pl.semaphore_signal(barrier, inc=1, device_id=dev, device_id_type=pl.DeviceIdType.MESH)
    pl.semaphore_wait(barrier, 7)

    def x_send(j):
        return rcopy(G.at[j, xhi, z, c], G.at[j, xhi, z, c], xs.at[j], xr.at[j], {"xhi": xh})

    def x_recv(j):
        return rcopy(G.at[j, xh, z, c], G.at[j, xh, z, c], xs.at[j], xr.at[j], {"xhi": xh})

    def unit(j, zz, cc):
        return G.at[j, :, zz, cc]

    def u_send(j, d):
        return rcopy(unit(j, z, c), unit(j, z, c), us.at[j, d], ur.at[j, d], {"z": (zp, zm)[d]})

    def u_recv(j, d):
        at = unit(j, (zm, zp)[d], c)
        return rcopy(at, at, us.at[j, d], ur.at[j, d], {"z": (zp, zm)[d]})

    def z_send(j, d):
        at = G.at[j, d, (zm, zp)[d], c]
        return rcopy(at, at, zs.at[j, d], zr.at[j, d], {"z": (zp, zm)[d]})

    def z_recv(j, d):
        at = G.at[j, d, z2, c]
        return rcopy(at, at, zs.at[j, d], zr.at[j, d], {"z": (zp, zm)[d]})

    slots = (z, zm, zp, z2)

    def c_send(j, s):
        at = unit(j, slots[s], c)
        return rcopy(at, at, cs.at[j, s], cr.at[j, s], {"core": co})

    def c_recv(j, s):
        at = unit(j, slots[s], co)
        return rcopy(at, at, cs.at[j, s], cr.at[j, s], {"core": co})

    top, low = pl.ds(0, 512), pl.ds(512, 512)
    wspec = (
        (W.at[0], W.at[2], {"y": yp}),
        (W.at[0], W.at[3], {"y": ym}),
        (W.at[0], W.at[1], {"xlo": xo}),
        (W.at[2, top], W.at[6, top], {"y": yp}),
        (W.at[3, low], W.at[6, low], {"y": ym}),
        (W.at[1], W.at[4], {"y": yp}),
        (W.at[1], W.at[5], {"y": ym}),
        (W.at[6], W.at[7], {"xlo": xo}),
    )

    def w_send(n):
        src, dst, dev = wspec[n]
        return rcopy(src, dst, ws.at[n], wr.at[n], dev)

    up, dn = pl.ds(0, 256), pl.ds(256, 256)
    rspec = (
        (S.at[0], RX.at[0], {"xlo": xo}),
        (S.at[1, up], RH.at[0], {"y": yp}),
        (S.at[1, dn], RH.at[1], {"y": ym}),
        (S.at[2], RP.at[0], {"y": yp}),
        (S.at[3], RP.at[1], {"y": ym}),
        (S.at[4], RY.at[0], {"y": yp}),
        (S.at[5], RY.at[1], {"y": ym}),
        (S.at[6], RX.at[1], {"xlo": xo}),
    )

    def r_send(n):
        src, dst, dev = rspec[n]
        return rcopy(src, dst, rs.at[n], rr.at[n], dev)

    def add_into(dst, rows, srcs):
        @pl.loop(0, rows // 64)
        def _(n):
            at = pl.ds(pl.multiple_of(n * 64, 64), 64)
            total = dst[at].astype(F32)
            for src in srcs:
                total = total + src[at].astype(F32)
            dst[at] = total.astype(BF)

    def weight_part(j):
        @pl.loop(0, 4)
        def _(n):
            at = pl.ds(pl.multiple_of(n * 256, 256), 256)
            rows = G[j, :, :, :, :, at].reshape(1024, 256)
            S[j, :, at] = dot(AT[...], rows).astype(BF)

    def att_part(j):
        @pl.loop(0, 2)
        def _(a):
            @pl.loop(0, 2)
            def _(b):
                at = pl.ds(pl.multiple_of((a * 2 + b) * 256, 256), 256)
                rows = G[j, a, pl.ds(b * 2, 2)].reshape(256, 1024)
                ACC[at] += dot(rows, W[7 - j])

    for j in range(8):
        own[j].wait()
        x_send(j).start()
    wcp.wait()
    for n in range(3):
        w_send(n).start()
    acp.wait()
    for h in range(4):
        AT[h * HD : (h + 1) * HD] = A[:, h * HD : (h + 1) * HD].T
    for cp in others:
        cp.wait()
    KT[...] = K[...].T
    ACC[...] = jnp.zeros_like(ACC)
    DK[...] = jnp.zeros_like(DK)
    DV[...] = jnp.zeros_like(DV)

    @pl.loop(0, 11)
    def _(i):
        @pl.when(i < 8)
        def _():
            x_recv(i).wait_recv()
            u_send(i, 0).start()
            u_send(i, 1).start()
            c_send(i, 0).start()

        @pl.when((i >= 1) & (i < 9))
        def _():
            j = i - 1
            for d in range(2):
                u_recv(j, d).wait_recv()
                z_send(j, d).start()
            c_send(j, 1).start()
            c_send(j, 2).start()

        @pl.when((i >= 2) & (i < 10))
        def _():
            j = i - 2
            for d in range(2):
                z_recv(j, d).wait_recv()
            c_send(j, 3).start()

        @pl.when(i >= 3)
        def _():
            j = i - 3
            for s in range(4):
                c_recv(j, s).wait_recv()
            weight_part(j)

        @pl.when(i == 3)
        def _():
            r_send(0).start()
            for n in range(3):
                w_send(n).wait_recv()
            for n in range(3, 7):
                w_send(n).start()

        @pl.when(i == 6)
        def _():
            for n in (3, 4):
                w_send(n).wait_recv()
            w_send(7).start()
            r_send(0).wait_recv()
            add_into(S.at[1], 512, [RX.at[0]])
            for n in range(1, 5):
                r_send(n).start()

        @pl.when(i >= 7)
        def _():
            att_part(i - 3)

    r_send(1).wait_recv()
    add_into(S.at[4, up], 256, [RH.at[0]])
    r_send(5).start()
    r_send(2).wait_recv()
    add_into(S.at[5, dn], 256, [RH.at[1]])
    r_send(6).start()

    w_send(5).wait_recv()
    w_send(6).wait_recv()

    @pl.loop(0, 4)
    def _(n):
        @pl.when(n == 3)
        def _():
            w_send(7).wait_recv()

        att_part(3 - n)

    for h in range(4):
        part = ACC[:, h * HD : (h + 1) * HD].astype(BF)
        GA[h] = part
        GAT[h] = part.T

    def r_mid():
        r_send(3).wait_recv()
        r_send(4).wait_recv()
        add_into(S.at[6], 512, [RP.at[0], RP.at[1]])
        r_send(7).start()

    @pl.loop(0, 4)
    def _(h):
        @pl.when(h == 2)
        def _():
            r_mid()

        for b in range(4):
            n = (b + 1) * 256
            lo = b * 256
            qb = Q[h, lo:n]
            gb = GA[h, lo:n]
            gt = GAT[h, :, lo:n]
            at_rows = AT[pl.ds(pl.multiple_of(h * HD, HD), HD), lo:n]
            offset = jnp.sum(gt.astype(F32) * at_rows.astype(F32), axis=0, keepdims=True)
            stat = ST[pl.ds(h, 1), lo:n]
            scores = dot(K[:n], qb, NT) * scale
            keys_at = lax.broadcasted_iota(jnp.int32, (n, 256), 0)
            query_at = lax.broadcasted_iota(jnp.int32, (n, 256), 1) + lo
            attention = jnp.where(keys_at <= query_at, jnp.exp(scores - stat), 0.0)
            DV[:n] += dot(attention.astype(BF), gb)
            grad_att = dot(V[:n], gb, NT)
            grad_scores = (attention * (grad_att - offset)).astype(BF)
            DK[:n] += dot(grad_scores, qb)
            dq = dot(KT[:, :n], grad_scores) * scale
            dq_out[lo:n, pl.ds(pl.multiple_of(h * HD, HD), HD)] = dq.T.astype(BF)

    zh = lax.rem(z, 2)
    dkt = (DK[...] * scale).T
    dvt = DV[...].T
    for n, full in enumerate((dkt, dvt)):
        for half in range(2):
            piece = full[half * 64 : half * 64 + 64]
            KF[n, half] = piece
            KB[half, n] = piece.astype(BF)
    k_send1 = rcopy(KB.at[1 - zh], KR1, ks.at[0], kr.at[0], {"z": zpair})
    k_send1.start()
    k_send1.wait_recv()
    for n in range(2):
        kept = KF[n, zh] + KR1[n].astype(F32)
        KF[n, 0] = kept
        KB2[0, n] = kept[:32].astype(BF)
        KB2[1, n] = kept[32:].astype(BF)
    k_send2 = rcopy(KB2.at[1 - c], KR2, ks.at[1], kr.at[1], {"core": co})
    k_send2.start()
    k_send2.wait_recv()
    for n in range(2):
        kv_out[n] = (KF[n, 0, pl.ds(pl.multiple_of(c * 32, 32), 32)] + KR2[n].astype(F32)).astype(BF)

    for n in (5, 6, 7):
        r_send(n).wait_recv()

    @pl.loop(0, 8)
    def _(n):
        at = pl.ds(pl.multiple_of(n * 64, 64), 64)
        total = S[7, at].astype(F32)
        for src in (RY.at[0], RY.at[1], RX.at[1]):
            total = total + src[at].astype(F32)
        wg_out[at] = total.astype(BF)

    @pl.loop(0, 8)
    def _(j):
        x_send(j).wait_send()
        for d in range(2):
            u_send(j, d).wait_send()
            z_send(j, d).wait_send()
        for s in range(4):
            c_send(j, s).wait_send()

    for n in range(8):
        w_send(n).wait_send()
        r_send(n).wait_send()
    k_send1.wait_send()
    k_send2.wait_send()


def per_device(grad_out, out_weight, query, keys, values, attended, stats):
    any_spec = pl.BlockSpec(memory_space=pl.ANY)
    vmem = pl.BlockSpec(memory_space=pltpu.VMEM)
    V_ = pltpu.VMEM
    dma = pltpu.SemaphoreType.DMA
    scratch = [
        V_((8, 2, 4, 2, 64, 1024), BF),
        V_((8, 1024, 512), BF),
        V_((8, 512, 1024), BF),
        V_((2, 512, 1024), BF),
        V_((2, 256, 1024), BF),
        V_((2, 512, 1024), BF),
        V_((2, 512, 1024), BF),
        V_((512, 1024), BF),
        V_((1024, 512), F32),
        V_((4, 1024, HD), BF),
        V_((4, 1024, HD), BF),
        V_((4, HD, 1024), BF),
        V_((1024, HD), BF),
        V_((1024, HD), BF),
        V_((HD, 1024), BF),
        V_((1024, 512), BF),
        V_((4, 1024), F32),
        V_((1024, HD), F32),
        V_((1024, HD), F32),
        V_((2, 2, 64, 1024), F32),
        V_((2, 2, 64, 1024), BF),
        V_((2, 64, 1024), BF),
        V_((2, 2, 32, 1024), BF),
        V_((2, 32, 1024), BF),
        dma((8,)), dma((8,)),
        dma((8, 2)), dma((8, 2)),
        dma((8, 2)), dma((8, 2)),
        dma((8, 4)), dma((8, 4)),
        dma((8,)), dma((8,)),
        dma((8,)), dma((8,)),
        dma((2,)), dma((2,)),
        dma((8,)), dma((9,)),
    ]
    dq, kv, wg = pl.pallas_call(
        kernel,
        out_shape=(
            jax.ShapeDtypeStruct((1024, 512), BF),
            jax.ShapeDtypeStruct((2, 32, 1024), BF),
            jax.ShapeDtypeStruct((512, 1024), BF),
        ),
        in_specs=[any_spec] * 7,
        out_specs=(vmem, vmem, vmem),
        scratch_shapes=scratch,
        compiler_params=pltpu.CompilerParams(
            collective_id=0, has_side_effects=True, vmem_limit_bytes=67_000_000
        ),
    )(grad_out, out_weight, query, keys, values, attended, stats)
    return (dq, kv[0].T, kv[1].T, wg.T)


def solution(mesh):
    torus = Mesh(mesh.devices.reshape(4, 2, 2, 4, 2), AXES)
    dp, tp = ("y", "xlo"), ("xhi", "z", "core")
    in_specs = (
        P(dp + tp, None),
        P(dp, tp),
        P(dp, tp),
        P(dp, None),
        P(dp, None),
        P(dp, tp),
        P(tp, dp),
    )
    out_specs = (P(dp, tp), P(dp, tp), P(dp, tp), P(dp, tp))
    return jax.shard_map(
        per_device, mesh=torus, in_specs=in_specs, out_specs=out_specs, check_vma=False
    )
```

time: 373 us -> 153 us (0.41)
  waiting for transfers between devices: 284 us -> 0 us
  Pallas kernels: 0 us -> 146 us
  matrix products: 67 us -> 0 us
  between operations: 14 us -> 0.64 us
    all_gather x3 -> x0, waiting for transfers between devices: 209 us -> none  [the longest x1 113 us: per_device(): grad_rows = lax.all_gather(grad_out, 'tensor', axis=0, tiled=True)]
    pallas_call x0 -> x1, Pallas kernels: none -> 146 us  [per_device(): pl.pallas_call(kernel, out_shape=(jax.ShapeDtypeStruct((1024, 512), BF),...]
    reduce_scatter x2 -> x0, waiting for transfers between devices: 68.3 us -> none  [sum_by_axis(): subtotal = lax.psum_scatter(subtotal, axis, scatter_dimension=0, tiled=True)]
    dot_general x7 -> x0, matrix products: 67 us -> none  [the longest x1 15.6 us: per_device(): jnp.dot(grad_block, gathered_by_axis(out_weight, DP, 0), preferred_elemen...]
    ppermute x2 -> x0, waiting for transfers between devices: 5.96 us -> none  [partner(): return lax.ppermute(value, axis, pairs)]
  transfers between devices with their start and end apart: 7 -> 0, of which waited for: 5 -> 0; matrix products, arithmetic and copies ran while one was open for 19% -> 0% of each run, Pallas kernels for 0% -> 0%
where the time goes in v1:
time: 153 us; the launch traced here: 151 us
  Pallas kernels  146 us (95%)
  local copies, waits for them, and re-layouts  4.86 us (3%)
    pallas_call x1, Pallas kernels, per_device(): pl.pallas_call(kernel, out_shape=(jax.ShapeDtypeStruct((1024, 512), BF),...  146 us
    unnamed x4, local copies, waits for them, and re-layouts  3.34 us

profile of v1, /device:TPU:1, one launch (start us, length us, event | category | flops | bytes accessed | tf_op | source)
XLA Modules:
  0.0 151.4 jit_solution(16097575622281436853)
XLA Ops:
  0.6 145.9 %shard_map.102 = (bf16[1024,512]{1,0:T(8,128)(2,1)}, bf16[2,32,1024]{2,1,0:T(8,128)(2,1)}, bf16[512,1024]{1,0:T(8,128)(2,1)}) custom-call(bf16[64,8192]{1,0:T(8,128)(2,1)} %g_in.1, bf16[1024,512]{1,0:T(8,128)(2,1)} %w_in.1, bf16[1024,512]{1,0:T(8,128)(2,1)} %q_in.1, bf16[1024,512]{1,0:T(8,128)(2,1)} %k_in.1, bf16[1024,512]{1,0:T(8,128)(2,1)} %v_in.1, ...), custom_call_target="tpu_custom_call" | custom-call | tf_op jit(solution)/shard_map/pallas_call | solution.py:383
  146.5 1.5 %slice_bitcast_fusion = (bf16[1024,32]{0,1:T(8,128)(2,1)}, bf16[1024,32]{0,1:T(8,128)(2,1)}) fusion(bf16[2,32,1024]{2,1,0:T(8,128)(2,1)} %get-tuple-element.8), kind=kLoop, calls=%fused_computation | loop fusion | bytes 262144 | tf_op jit(solution)/shard_map/transpose | solution.py:397
  148.1 0.0 copy-start
  148.1 2.4 %copy.11 = bf16[1024,512]{1,0:T(8,128)(2,1)} copy(bf16[1024,512]{0,1:T(8,128)(2,1)} %bitcast.9) | data formatting | bytes 2097152
  150.4 0.0 copy-done
  150.4 1.0 copy.13
Async XLA Ops:
  148.1 2.4 %copy-start = (bf16[1024,512]{1,0:T(8,128)(2,1)S(1)}, bf16[1024,512]{1,0:T(8,128)(2,1)}, u32[]{:S(2)}) copy-start(bf16[1024,512]{1,0:T(8,128)(2,1)} %get-tuple-element.20) | copy-start | bytes 3145732

commit v2 on v1

--- a/solution.py
+++ b/solution.py
@@ -34,12 +34,13 @@
     g_in, w_in, q_in, k_in, v_in, a_in, st_in,
     dq_out, kv_out, wg_out,
     G, W, S, RX, RH, RP, RY, AT, ACC, Q, GA, GAT, K, V, KT, A, ST,
-    DK, DV, KF, KB, KR1, KB2, KR2,
+    P0, P1, P2, P3, DK, DV, KF, KB, KR1, KB2, KR2,
     xs, xr, us, ur, zs, zr, cs, cr, ws, wr, rs, rr, ks, kr, ls, lq,
 ):
     y, xlo, xhi = lax.axis_index("y"), lax.axis_index("xlo"), lax.axis_index("xhi")
     z, c = lax.axis_index("z"), lax.axis_index("core")
     scale = HD ** (-0.5)
+    PT = (P0, P1, P2, P3)
     yp, ym, y2 = lax.rem(y + 1, 4), lax.rem(y + 3, 4), lax.rem(y + 2, 4)
     zp, zm, z2 = lax.rem(z + 1, 4), lax.rem(z + 3, 4), lax.rem(z + 2, 4)
     xo, xh, co = 1 - xlo, 1 - xhi, 1 - c
@@ -85,12 +86,13 @@
     def unit(j, zz, cc):
         return G.at[j, :, zz, cc]
 
-    def u_send(j, d):
-        return rcopy(unit(j, z, c), unit(j, z, c), us.at[j, d], ur.at[j, d], {"z": (zp, zm)[d]})
-
-    def u_recv(j, d):
-        at = unit(j, (zm, zp)[d], c)
-        return rcopy(at, at, us.at[j, d], ur.at[j, d], {"z": (zp, zm)[d]})
+    def u_send(j, d, p):
+        at = G.at[j, (xhi, xh)[p], z, c]
+        return rcopy(at, at, us.at[j, d, p], ur.at[j, d, p], {"z": (zp, zm)[d]})
+
+    def u_recv(j, d, p):
+        at = G.at[j, (xhi, xh)[p], (zm, zp)[d], c]
+        return rcopy(at, at, us.at[j, d, p], ur.at[j, d, p], {"z": (zp, zm)[d]})
 
     def z_send(j, d):
         at = G.at[j, d, (zm, zp)[d], c]
@@ -112,14 +114,20 @@
 
     top, low = pl.ds(0, 512), pl.ds(512, 512)
     wspec = (
-        (W.at[0], W.at[2], {"y": yp}),
-        (W.at[0], W.at[3], {"y": ym}),
-        (W.at[0], W.at[1], {"xlo": xo}),
+        (W.at[0, top], W.at[2, top], {"y": yp}),
+        (W.at[0, low], W.at[3, low], {"y": ym}),
+        (W.at[0, low], W.at[2, low], {"y": yp}),
+        (W.at[0, top], W.at[3, top], {"y": ym}),
+        (W.at[0, top], W.at[1, top], {"xlo": xo}),
+        (W.at[0, low], W.at[1, low], {"xlo": xo}),
         (W.at[2, top], W.at[6, top], {"y": yp}),
         (W.at[3, low], W.at[6, low], {"y": ym}),
-        (W.at[1], W.at[4], {"y": yp}),
-        (W.at[1], W.at[5], {"y": ym}),
-        (W.at[6], W.at[7], {"xlo": xo}),
+        (W.at[1, top], W.at[4, top], {"y": yp}),
+        (W.at[1, top], W.at[5, top], {"y": ym}),
+        (W.at[1, low], W.at[4, low], {"y": yp}),
+        (W.at[1, low], W.at[5, low], {"y": ym}),
+        (W.at[6, top], W.at[7, top], {"xlo": xo}),
+        (W.at[6, low], W.at[7, low], {"xlo": xo}),
     )
 
     def w_send(n):
@@ -133,8 +141,10 @@
         (S.at[1, dn], RH.at[1], {"y": ym}),
         (S.at[2], RP.at[0], {"y": yp}),
         (S.at[3], RP.at[1], {"y": ym}),
-        (S.at[4], RY.at[0], {"y": yp}),
-        (S.at[5], RY.at[1], {"y": ym}),
+        (S.at[4, dn], RY.at[0, dn], {"y": yp}),
+        (S.at[5, up], RY.at[1, up], {"y": ym}),
+        (S.at[4, up], RY.at[0, up], {"y": yp}),
+        (S.at[5, dn], RY.at[1, dn], {"y": ym}),
         (S.at[6], RX.at[1], {"xlo": xo}),
     )
 
@@ -167,12 +177,29 @@
                 rows = G[j, a, pl.ds(b * 2, 2)].reshape(256, 1024)
                 ACC[at] += dot(rows, W[7 - j])
 
-    for j in range(8):
-        own[j].wait()
+    def w_start(*which):
+        for n in which:
+            w_send(n).start()
+
+    def w_wait(*which):
+        for n in which:
+            w_send(n).wait_recv()
+
+    for cp in own:
+        cp.wait()
+    wcp.wait()
+    for j in range(2):
+        for d in range(2):
+            u_send(j, d, 0).start()
+    w_start(0, 1, 2, 3)
+    for j in range(4):
         x_send(j).start()
-    wcp.wait()
-    for n in range(3):
-        w_send(n).start()
+    w_start(4)
+    for j in range(4, 6):
+        x_send(j).start()
+    w_start(5)
+    for j in range(6, 8):
+        x_send(j).start()
     acp.wait()
     for h in range(4):
         AT[h * HD : (h + 1) * HD] = A[:, h * HD : (h + 1) * HD].T
@@ -183,23 +210,70 @@
     DK[...] = jnp.zeros_like(DK)
     DV[...] = jnp.zeros_like(DV)
 
+    def spans(b):
+        n, lo = (b + 1) * 256, b * 256
+        return n, lo
+
+    def prob_part(h):
+        for b in range(4):
+            n, lo = spans(b)
+            scores = dot(K[:n], Q[h, lo:n], NT) * scale
+            keys_at = lax.broadcasted_iota(jnp.int32, (n, 256), 0)
+            query_at = lax.broadcasted_iota(jnp.int32, (n, 256), 1) + lo
+            stat = ST[pl.ds(h, 1), lo:n]
+            PT[b][h] = jnp.where(keys_at <= query_at, jnp.exp(scores - stat), 0.0).astype(BF)
+
     @pl.loop(0, 11)
     def _(i):
         @pl.when(i < 8)
         def _():
             x_recv(i).wait_recv()
-            u_send(i, 0).start()
-            u_send(i, 1).start()
+            u_send(i, 0, 1).start()
+            u_send(i, 1, 1).start()
             c_send(i, 0).start()
+
+        @pl.when(i >= 3)
+        def _():
+            j = i - 3
+            for s in range(4):
+                c_recv(j, s).wait_recv()
+            weight_part(j)
+
+        @pl.when(i == 3)
+        def _():
+            r_send(0).start()
+
+        @pl.when(i == 5)
+        def _():
+            r_send(3).start()
+
+        @pl.when(i == 6)
+        def _():
+            r_send(4).start()
+
+        @pl.when((i >= 1) & (i < 5))
+        def _():
+            prob_part(i - 1)
 
         @pl.when((i >= 1) & (i < 9))
         def _():
             j = i - 1
             for d in range(2):
-                u_recv(j, d).wait_recv()
+                u_recv(j, d, 0).wait_recv()
+                u_recv(j, d, 1).wait_recv()
                 z_send(j, d).start()
             c_send(j, 1).start()
             c_send(j, 2).start()
+
+        @pl.when(i < 6)
+        def _():
+            for d in range(2):
+                u_send(i + 2, d, 0).start()
+
+        @pl.when(i == 2)
+        def _():
+            w_wait(0, 1)
+            w_start(6, 7)
 
         @pl.when((i >= 2) & (i < 10))
         def _():
@@ -208,52 +282,44 @@
                 z_recv(j, d).wait_recv()
             c_send(j, 3).start()
 
-        @pl.when(i >= 3)
-        def _():
-            j = i - 3
-            for s in range(4):
-                c_recv(j, s).wait_recv()
-            weight_part(j)
-
         @pl.when(i == 3)
         def _():
-            r_send(0).start()
-            for n in range(3):
-                w_send(n).wait_recv()
-            for n in range(3, 7):
-                w_send(n).start()
-
-        @pl.when(i == 6)
-        def _():
-            for n in (3, 4):
-                w_send(n).wait_recv()
-            w_send(7).start()
+            w_wait(4)
+            w_start(8, 9)
+
+        @pl.when(i == 4)
+        def _():
+            w_wait(2, 3, 6, 7)
+            w_start(12, 13)
+            w_wait(5)
+            w_start(10, 11)
+
+        @pl.when(i == 8)
+        def _():
+            w_wait(8, 9, 10, 11)
+
+        @pl.when(i >= 7)
+        def _():
+            att_part(i - 3)
+
+        @pl.when((i >= 7) & (i < 10))
+        def _():
+            att_part(i - 6)
+
+        @pl.when(i == 9)
+        def _():
             r_send(0).wait_recv()
             add_into(S.at[1], 512, [RX.at[0]])
-            for n in range(1, 5):
+            for n in (1, 2, 5, 6):
                 r_send(n).start()
 
-        @pl.when(i >= 7)
-        def _():
-            att_part(i - 3)
-
-    r_send(1).wait_recv()
-    add_into(S.at[4, up], 256, [RH.at[0]])
-    r_send(5).start()
-    r_send(2).wait_recv()
-    add_into(S.at[5, dn], 256, [RH.at[1]])
-    r_send(6).start()
-
-    w_send(5).wait_recv()
-    w_send(6).wait_recv()
-
-    @pl.loop(0, 4)
-    def _(n):
-        @pl.when(n == 3)
-        def _():
-            w_send(7).wait_recv()
-
-        att_part(3 - n)
+    r_send(3).wait_recv()
+    r_send(4).wait_recv()
+    add_into(S.at[6], 512, [RP.at[0], RP.at[1]])
+    r_send(9).start()
+
+    w_wait(12, 13)
+    att_part(0)
 
     for h in range(4):
         part = ACC[:, h * HD : (h + 1) * HD].astype(BF)
@@ -261,33 +327,30 @@
         GAT[h] = part.T
 
     def r_mid():
-        r_send(3).wait_recv()
-        r_send(4).wait_recv()
-        add_into(S.at[6], 512, [RP.at[0], RP.at[1]])
+        r_send(1).wait_recv()
+        add_into(S.at[4, up], 256, [RH.at[0]])
         r_send(7).start()
+        r_send(2).wait_recv()
+        add_into(S.at[5, dn], 256, [RH.at[1]])
+        r_send(8).start()
 
     @pl.loop(0, 4)
     def _(h):
-        @pl.when(h == 2)
+        @pl.when(h == 1)
         def _():
             r_mid()
 
         for b in range(4):
-            n = (b + 1) * 256
-            lo = b * 256
+            n, lo = spans(b)
             qb = Q[h, lo:n]
             gb = GA[h, lo:n]
             gt = GAT[h, :, lo:n]
             at_rows = AT[pl.ds(pl.multiple_of(h * HD, HD), HD), lo:n]
             offset = jnp.sum(gt.astype(F32) * at_rows.astype(F32), axis=0, keepdims=True)
-            stat = ST[pl.ds(h, 1), lo:n]
-            scores = dot(K[:n], qb, NT) * scale
-            keys_at = lax.broadcasted_iota(jnp.int32, (n, 256), 0)
-            query_at = lax.broadcasted_iota(jnp.int32, (n, 256), 1) + lo
-            attention = jnp.where(keys_at <= query_at, jnp.exp(scores - stat), 0.0)
-            DV[:n] += dot(attention.astype(BF), gb)
+            attention = PT[b][h]
+            DV[:n] += dot(attention, gb)
             grad_att = dot(V[:n], gb, NT)
-            grad_scores = (attention * (grad_att - offset)).astype(BF)
+            grad_scores = (attention.astype(F32) * (grad_att - offset)).astype(BF)
             DK[:n] += dot(grad_scores, qb)
             dq = dot(KT[:, :n], grad_scores) * scale
             dq_out[lo:n, pl.ds(pl.multiple_of(h * HD, HD), HD)] = dq.T.astype(BF)
@@ -314,7 +377,7 @@
     for n in range(2):
         kv_out[n] = (KF[n, 0, pl.ds(pl.multiple_of(c * 32, 32), 32)] + KR2[n].astype(F32)).astype(BF)
 
-    for n in (5, 6, 7):
+    for n in (5, 6, 7, 8, 9):
         r_send(n).wait_recv()
 
     @pl.loop(0, 8)
@@ -329,16 +392,26 @@
     def _(j):
         x_send(j).wait_send()
         for d in range(2):
-            u_send(j, d).wait_send()
+            u_send(j, d, 0).wait_send()
+            u_send(j, d, 1).wait_send()
             z_send(j, d).wait_send()
         for s in range(4):
             c_send(j, s).wait_send()
 
-    for n in range(8):
+    for n in range(14):
         w_send(n).wait_send()
+    for n in range(10):
         r_send(n).wait_send()
     k_send1.wait_send()
     k_send2.wait_send()
+
+
+def finish(dq_in, kv_in, wg_in, dq_out, dk_out, dv_out, wg_out):
+    for n in range(4):
+        wg_out[:, n * HD : (n + 1) * HD] = wg_in[n * HD : (n + 1) * HD].T
+    dq_out[...] = dq_in[...]
+    dk_out[...] = kv_in[0]
+    dv_out[...] = kv_in[1]
 
 
 def per_device(grad_out, out_weight, query, keys, values, attended, stats):
@@ -364,6 +437,10 @@
         V_((HD, 1024), BF),
         V_((1024, 512), BF),
         V_((4, 1024), F32),
+        V_((4, 256, 256), BF),
+        V_((4, 512, 256), BF),
+        V_((4, 768, 256), BF),
+        V_((4, 1024, 256), BF),
         V_((1024, HD), F32),
         V_((1024, HD), F32),
         V_((2, 2, 64, 1024), F32),
@@ -372,11 +449,11 @@
         V_((2, 2, 32, 1024), BF),
         V_((2, 32, 1024), BF),
         dma((8,)), dma((8,)),
-        dma((8, 2)), dma((8, 2)),
+        dma((8, 2, 2)), dma((8, 2, 2)),
         dma((8, 2)), dma((8, 2)),
         dma((8, 4)), dma((8, 4)),
-        dma((8,)), dma((8,)),
-        dma((8,)), dma((8,)),
+        dma((14,)), dma((14,)),
+        dma((10,)), dma((10,)),
         dma((2,)), dma((2,)),
         dma((8,)), dma((9,)),
     ]
@@ -394,7 +471,18 @@
             collective_id=0, has_side_effects=True, vmem_limit_bytes=67_000_000
         ),
     )(grad_out, out_weight, query, keys, values, attended, stats)
-    return (dq, kv[0].T, kv[1].T, wg.T)
+    dq, dk, dv, wg = pl.pallas_call(
+        finish,
+        out_shape=(
+            jax.ShapeDtypeStruct((1024, 512), BF),
+            jax.ShapeDtypeStruct((32, 1024), BF),
+            jax.ShapeDtypeStruct((32, 1024), BF),
+            jax.ShapeDtypeStruct((1024, 512), BF),
+        ),
+        in_specs=[vmem] * 3,
+        out_specs=(vmem,) * 4,
+    )(dq, kv, wg)
+    return (dq, dk.T, dv.T, wg)
 
 
 def solution(mesh):

time: 153 us -> 129 us (0.84)
  Pallas kernels: 146 us -> 127 us
  local copies, waits for them, and re-layouts: 4.86 us -> 0 us
    pallas_call x1, Pallas kernels: 146 us -> 124 us  [per_device(): pl.pallas_call(kernel, out_shape=(jax.ShapeDtypeStruct((1024, 512), BF),...]
    unnamed x4 -> x0, local copies, waits for them, and re-layouts: 3.34 us -> none
    pallas_call x0 -> x1, Pallas kernels: none -> 3.3 us  [per_device(): pl.pallas_call(finish, out_shape=(jax.ShapeDtypeStruct((1024, 512), BF),...]
where the time goes in v2:
time: 129 us; the launch traced here: 128 us
  Pallas kernels  127 us (98%)
    pallas_call x1, Pallas kernels, per_device(): pl.pallas_call(kernel, out_shape=(jax.ShapeDtypeStruct((1024, 512), BF),...  124 us
    pallas_call x1, Pallas kernels, per_device(): pl.pallas_call(finish, out_shape=(jax.ShapeDtypeStruct((1024, 512), BF),...  3.3 us

profile of v2, /device:TPU:1, one launch (start us, length us, event | category | flops | bytes accessed | tf_op | source)
XLA Modules:
  0.0 127.7 jit_solution(8621459201473884517)
XLA Ops:
  0.6 123.7 %shard_map.102 = (bf16[1024,512]{1,0:T(8,128)(2,1)}, bf16[2,32,1024]{2,1,0:T(8,128)(2,1)}, bf16[512,1024]{1,0:T(8,128)(2,1)}) custom-call(bf16[64,8192]{1,0:T(8,128)(2,1)} %g_in.1, bf16[1024,512]{1,0:T(8,128)(2,1)} %w_in.1, bf16[1024,512]{1,0:T(8,128)(2,1)} %q_in.1, bf16[1024,512]{1,0:T(8,128)(2,1)} %k_in.1, bf16[1024,512]{1,0:T(8,128)(2,1)} %v_in.1, ...), custom_call_target="tpu_custom_call" | custom-call | tf_op jit(solution)/shard_map/pallas_call | solution.py:460
  124.4 3.3 %shard_map.103 = (bf16[1024,512]{1,0:T(8,128)(2,1)}, bf16[32,1024]{1,0:T(8,128)(2,1)}, bf16[32,1024]{1,0:T(8,128)(2,1)}, bf16[1024,512]{1,0:T(8,128)(2,1)}) custom-call(bf16[1024,512]{1,0:T(8,128)(2,1)} %get-tuple-element.11.dq_in, bf16[2,32,1024]{2,1,0:T(8,128)(2,1)} %get-tuple-element.12.kv_in, bf16[512,1024]{1,0:T(8,128)(2,1)} %get-tuple-element.13.wg_in), custom_call_target="tpu_custom_call" | custom-call | tf_op jit(solution)/shard_map/pallas_call | solution.py:474

commit v3 on v1

v3 whole, which is shorter than its diff:
```python
import jax
import jax.numpy as jnp
from jax import lax
from jax.experimental import pallas as pl
from jax.experimental.pallas import tpu as pltpu
from jax.sharding import Mesh
from jax.sharding import PartitionSpec as P

HD = 128
GROUP = 16
BF = jnp.bfloat16
F32 = jnp.float32
AXES = ("y", "xlo", "xhi", "z", "core")
NN = (((1,), (0,)), ((), ()))
NT = (((1,), (1,)), ((), ()))


def dot(a, b, dims=NN):
    return lax.dot_general(a, b, dims, preferred_element_type=F32)


def rcopy(src, dst, send, recv, dev):
    return pltpu.make_async_remote_copy(
        src_ref=src,
        dst_ref=dst,
        send_sem=send,
        recv_sem=recv,
        device_id=dev,
        device_id_type=pl.DeviceIdType.MESH,
    )


def kernel(
    g_in, w_in, q_in, k_in, v_in, a_in, st_in,
    dq_out, dk_out, dv_out, wg_out,
    G, W, S, RH, RY, AT, AT2, ACC, PG, PS, PR, Q, GA, OFF, K, V, KT, ST,
    P0, P1, P2, P3, DQ, KF, KB, KS, KR1, KB2, KR2,
    xs, xr, es, er, us, ur, zs, zr, cs, cr, ws, wr, rs, rr, ats, atr, ps, pr, ks, kr, ls,
):
    y, xlo, xhi = lax.axis_index("y"), lax.axis_index("xlo"), lax.axis_index("xhi")
    z, c = lax.axis_index("z"), lax.axis_index("core")
    scale = HD ** (-0.5)
    PT = (P0, P1, P2, P3)
    yp, ym, y2 = lax.rem(y + 1, 4), lax.rem(y + 3, 4), lax.rem(y + 2, 4)
    zp, zm, z2 = lax.rem(z + 1, 4), lax.rem(z + 3, 4), lax.rem(z + 2, 4)
    xo, xh, co = 1 - xlo, 1 - xhi, 1 - c
    zpair = z + 1 - 2 * lax.rem(z, 2)

    head = xhi * 2 + z // 2
    hcol = pl.ds(pl.multiple_of(head * HD, HD), HD)
    blocks = (y2, yp, ym, y)
    own_chunk = (0, 5, 6, 7)
    pair_chunk = (1, 2, 3, 4)

    def columns(q, x):
        return pl.ds(pl.multiple_of((blocks[q] * 2 + x) * 1024, 1024), 1024)

    for q in range(4):
        pltpu.make_async_copy(
            g_in.at[:, columns(q, xlo)], G.at[own_chunk[q], xhi, z, c], ls.at[0]
        ).start()
    wcp = pltpu.make_async_copy(w_in, W.at[0], ls.at[1])
    wcp.start()
    for h in range(4):
        pltpu.make_async_copy(a_in.at[:, h * HD : (h + 1) * HD], GA.at[h], ls.at[2]).start()
        pltpu.make_async_copy(q_in.at[:, h * HD : (h + 1) * HD], Q.at[h], ls.at[3]).start()
    others = [
        pltpu.make_async_copy(k_in.at[:, hcol], K, ls.at[4]),
        pltpu.make_async_copy(v_in.at[:, hcol], V, ls.at[5]),
        pltpu.make_async_copy(st_in, ST, ls.at[6]),
    ]
    for cp in others:
        cp.start()

    barrier = pltpu.get_barrier_semaphore()
    for dev in ({"y": yp}, {"y": ym}, {"xlo": xo}, {"xhi": xh}, {"z": zp}, {"z": zm}, {"core": co}):
        pl.semaphore_signal(barrier, inc=1, device_id=dev, device_id_type=pl.DeviceIdType.MESH)
    pl.semaphore_wait(barrier, 7)

    def e_send(q):
        dst = G.at[pair_chunk[q], xhi, z, c]
        return rcopy(g_in.at[:, columns(q, xo)], dst, es, er.at[q], {"xlo": xo})

    def e_recv(q):
        dst = G.at[pair_chunk[q], xhi, z, c]
        return rcopy(dst, dst, es, er.at[q], {"xlo": xo})

    def x_send(j):
        return rcopy(G.at[j, xhi, z, c], G.at[j, xhi, z, c], xs, xr.at[j], {"xhi": xh})

    def x_recv(j):
        return rcopy(G.at[j, xh, z, c], G.at[j, xh, z, c], xs, xr.at[j], {"xhi": xh})

    def unit(j, zz, cc):
        return G.at[j, :, zz, cc]

    def u_send(j, d, p):
        at = G.at[j, (xhi, xh)[p], z, c]
        return rcopy(at, at, us, ur.at[j, d], {"z": (zp, zm)[d]})

    def u_recv(j, d):
        at = unit(j, (zm, zp)[d], c)
        return rcopy(at, at, us, ur.at[j, d], {"z": (zp, zm)[d]})

    def z_send(j, d):
        at = G.at[j, d, (zm, zp)[d], c]
        return rcopy(at, at, zs, zr.at[j], {"z": (zp, zm)[d]})

    def z_recv(j):
        at = unit(j, z2, c)
        return rcopy(at, at, zs, zr.at[j], {"z": zp})

    slots = (z, zm, zp, z2)

    def c_send(j, s):
        at = unit(j, slots[s], c)
        return rcopy(at, at, cs, cr.at[j], {"core": co})

    def c_recv(j):
        at = G.at[j, :, :, co]
        return rcopy(at, at, cs, cr.at[j], {"core": co})

    top, low = pl.ds(0, 512), pl.ds(512, 512)
    wspec = (
        (W.at[0, top], W.at[1, top], {"y": yp}),
        (W.at[0, low], W.at[2, low], {"y": ym}),
        (W.at[0, low], W.at[1, low], {"y": yp}),
        (W.at[0, top], W.at[2, top], {"y": ym}),
        (W.at[1, top], W.at[3, top], {"y": yp}),
        (W.at[2, low], W.at[3, low], {"y": ym}),
    )

    def w_send(n):
        src, dst, dev = wspec[n]
        return rcopy(src, dst, ws, wr.at[n], dev)

    up, dn = pl.ds(0, 256), pl.ds(256, 256)
    rspec = (
        (S.at[0, up], RH.at[0], {"y": yp}),
        (S.at[0, dn], RH.at[1], {"y": ym}),
        (S.at[1, dn], RY.at[0, dn], {"y": yp}),
        (S.at[1, up], RY.at[0, up], {"y": yp}),
        (S.at[2, up], RY.at[1, up], {"y": ym}),
        (S.at[2, dn], RY.at[1, dn], {"y": ym}),
    )

    def r_send(n):
        src, dst, dev = rspec[n]
        return rcopy(src, dst, rs, rr.at[n], dev)

    def a_send(h):
        at = pl.ds(h * HD, HD)
        return rcopy(AT.at[at], AT2.at[at], ats, atr.at[h], {"xlo": xo})

    def p_send():
        return rcopy(PS, PR, ps, pr, {"xlo": xo})

    def add_into(dst, rows, srcs):
        @pl.loop(0, rows // 64)
        def _(n):
            at = pl.ds(pl.multiple_of(n * 64, 64), 64)
            total = dst[at].astype(F32)
            for src in srcs:
                total = total + src[at].astype(F32)
            dst[at] = total.astype(BF)

    def weight_part(q, rows):
        @pl.loop(0, 4)
        def _(n):
            at = pl.ds(pl.multiple_of(n * 256, 256), 256)
            mine = G[own_chunk[q], :, :, :, :, at].reshape(1024, 256)
            pair = G[pair_chunk[q], :, :, :, :, at].reshape(1024, 256)
            S[q, rows, at] = (dot(AT[rows], mine) + dot(AT2[rows], pair)).astype(BF)

    def att_part(acc, j, slot):
        @pl.loop(0, 2)
        def _(a):
            @pl.loop(0, 2)
            def _(b):
                at = pl.ds(pl.multiple_of((a * 2 + b) * 256, 256), 256)
                rows = G[j, a, pl.ds(b * 2, 2)].reshape(256, 1024)
                acc[at] += dot(rows, W[slot])

    def w_start(*which):
        for n in which:
            w_send(n).start()

    def w_wait(*which):
        for n in which:
            w_send(n).wait_recv()

    first = G.at[pl.ds(0, 4), 0, 0, 0]
    pltpu.make_async_copy(first, first, ls.at[0]).wait()
    wcp.wait()
    for d in range(2):
        u_send(0, d, 0).start()
    w_start(0, 1, 2, 3)
    x_send(0).start()
    e_send(0).start()
    e_send(1).start()
    pltpu.make_async_copy(GA, GA, ls.at[2]).wait()
    for h in range(4):
        AT[h * HD : (h + 1) * HD] = GA[h].T
    pltpu.make_async_copy(Q, Q, ls.at[3]).wait()
    for cp in others:
        cp.wait()
    KT[...] = K[...].T
    ACC[...] = jnp.zeros_like(ACC)
    PG[...] = jnp.zeros_like(PG)

    def prob_part(h):
        stat = ST[pl.ds(h, 1)]
        for r in range(4):
            lo = r * 256
            n = 1024 - lo
            scores = dot(K[lo : lo + 256], Q[h, lo:], NT) * scale
            keys_at = lax.broadcasted_iota(jnp.int32, (256, n), 0)
            query_at = lax.broadcasted_iota(jnp.int32, (256, n), 1)
            value = jnp.exp(scores - stat[:, lo:])
            PT[r][h] = jnp.where(keys_at <= query_at, value, 0.0).astype(BF)

    def at_step(i, n, run):
        @pl.when(i == n)
        def _():
            run()

    @pl.loop(0, 11)
    def _(i):
        @pl.when(i < 8)
        def _():
            x_recv(i).wait_recv()
            u_send(i, 0, 1).start()
            u_send(i, 1, 1).start()
            c_send(i, 0).start()

        def feed(q):
            e_recv(q).wait_recv()
            x_send(q + 1).start()
            for d in range(2):
                u_send(q + 1, d, 0).start()

        def feed_0():
            feed(0)
            e_send(2).start()

        def feed_1():
            feed(1)
            e_send(3).start()
            a_send(0).start()

        def feed_2():
            feed(2)
            a_send(1).start()

        def feed_3():
            feed(3)
            a_send(2).start()
            x_send(5).start()

        def feed_4():
            a_send(3).start()
            x_send(6).start()

        def feed_5():
            x_send(7).start()

        for n, run in enumerate((feed_0, feed_1, feed_2, feed_3, feed_4, feed_5)):
            at_step(i, n, run)

        @pl.when(i >= 3)
        def _():
            c_recv(i - 3).wait_recv()

        def pair_done():
            att_part(PG, 4, 0)
            PS[...] = PG[...].astype(BF)
            p_send().start()

        at_step(i, 7, pair_done)

        @pl.when((i >= 1) & (i < 5))
        def _():
            prob_part(i - 1)

        @pl.when((i >= 1) & (i < 9))
        def _():
            j = i - 1
            for d in range(2):
                u_recv(j, d).wait_recv()
                z_send(j, d).start()
            c_send(j, 1).start()
            c_send(j, 2).start()

        @pl.when((i >= 4) & (i < 7))
        def _():
            for d in range(2):
                u_send(i + 1, d, 0).start()

        def relay_w():
            w_wait(0, 1)
            w_start(4, 5)

        at_step(i, 2, relay_w)

        @pl.when((i >= 2) & (i < 10))
        def _():
            j = i - 2
            z_recv(j).wait_recv()
            c_send(j, 3).start()

        def step_4():
            w_wait(2, 3, 4, 5)
            att_part(ACC, 0, 3)

        def step_5():
            a_send(0).wait_recv()
            a_send(1).wait_recv()
            weight_part(0, up)
            r_send(0).start()
            att_part(PG, 1, 3)
            att_part(PG, 2, 2)

        def step_6():
            att_part(PG, 3, 1)
            a_send(2).wait_recv()
            a_send(3).wait_recv()
            weight_part(0, dn)
            r_send(1).start()

        def step_8():
            weight_part(1, pl.ds(0, 512))
            r_send(2).start()
            r_send(0).wait_recv()
            add_into(S.at[1, up], 256, [RH.at[0]])
            r_send(3).start()
            att_part(ACC, 5, 2)

        def step_9():
            weight_part(2, pl.ds(0, 512))
            r_send(4).start()
            r_send(1).wait_recv()
            add_into(S.at[2, dn], 256, [RH.at[1]])
            r_send(5).start()
            att_part(ACC, 6, 1)

        def step_10():
            att_part(ACC, 7, 0)
            weight_part(3, pl.ds(0, 512))

        for n, run in ((4, step_4), (5, step_5), (6, step_6), (8, step_8), (9, step_9), (10, step_10)):
            at_step(i, n, run)

    p_send().wait_recv()
    for h in range(4):
        cols = slice(h * HD, (h + 1) * HD)
        part = (ACC[:, cols] + PR[:, cols].astype(F32)).astype(BF)
        GA[h] = part
        both = part.T.astype(F32) * AT[h * HD : (h + 1) * HD].astype(F32)
        OFF[h : h + 1] = jnp.sum(both, axis=0, keepdims=True)

    zh = lax.rem(z, 2)

    def kv_first(r):
        return rcopy(KB.at[r, :, :, 1 - c], KR1.at[r], ks.at[0], kr.at[0, r], {"core": co})

    def kv_second(r):
        return rcopy(KB2.at[r, 1 - zh], KR2.at[r], ks.at[1], kr.at[1, r], {"z": zpair})

    def kv_middle(r):
        kv_first(r).wait_recv()
        for n in range(2):
            for half in range(2):
                total = KF[r, n, half, c] + KR1[r, n, half].astype(F32)
                KS[r, n, half] = total
                KB2[r, half, n] = total.astype(BF)
        kv_second(r).start()

    for r in range(4):
        lo = r * 256
        mine = slice(lo, lo + 256)
        dv = jnp.zeros((256, HD), F32)
        dk = jnp.zeros((256, HD), F32)
        for h in range(4):
            attention = PT[r][h]
            gb = GA[h, lo:]
            dv = dv + dot(attention, gb)
            grad_att = dot(V[mine], gb, NT)
            grad_scores = (attention.astype(F32) * (grad_att - OFF[h : h + 1, lo:])).astype(BF)
            dk = dk + dot(grad_scores, Q[h, lo:])
            dq = dot(KT[:, mine], grad_scores)
            if r > 0:
                dq = dq + DQ[h, :, lo:]
            DQ[h, :, lo:] = dq
            dq_out[mine, h * HD : (h + 1) * HD] = (dq[:, :256] * scale).T.astype(BF)
        for n, full in enumerate(((dk * scale).T, dv.T)):
            for half in range(2):
                for core in range(2):
                    at = half * 64 + core * 32
                    KF[r, n, half, core] = full[at : at + 32]
                    KB[r, n, half, core] = full[at : at + 32].astype(BF)
        kv_first(r).start()
        if r > 0:
            kv_middle(r - 1)
    kv_middle(3)
    for r in range(4):
        kv_second(r).wait_recv()
        for n in range(2):
            total = KS[r, n, zh] + KR2[r, n].astype(F32)
            (dk_out, dv_out)[n][:, r * 256 : r * 256 + 256] = total.astype(BF)

    r_send(2).wait_recv()
    r_send(3).wait_recv()
    for n in range(4):
        at = slice(n * HD, (n + 1) * HD)
        ACC[:, at] = (S[3, at].astype(F32) + RY[0, at].astype(F32)).T
    for n in range(4):
        at = slice(n * HD, (n + 1) * HD)
        if n % 2 == 0:
            r_send(4 + n // 2).wait_recv()
        wg_out[:, at] = (ACC[:, at] + RY[1, at].T.astype(F32)).astype(BF)

    for ref, sem in (
        (first, es),
        (G.at[:, 0, 0, 0], xs),
        (G.at[pl.ds(0, 2)], us),
        (G.at[0], zs),
        (G.at[pl.ds(0, 4)], cs),
        (W.at[pl.ds(0, 3)], ws),
        (S.at[pl.ds(0, 3)], rs),
        (AT, ats),
        (PS, ps),
        (KR1, ks.at[0]),
        (KR2, ks.at[1]),
    ):
        rcopy(ref, ref, sem, sem, {"core": co}).wait_send()


def finish(*refs):
    sems = refs[8]
    copies = [pltpu.make_async_copy(refs[n], refs[4 + n], sems.at[n]) for n in range(4)]
    for cp in copies:
        cp.start()
    for cp in copies:
        cp.wait()


def per_device(grad_out, out_weight, query, keys, values, attended, stats):
    any_spec = pl.BlockSpec(memory_space=pl.ANY)
    vmem = pl.BlockSpec(memory_space=pltpu.VMEM)
    V_ = pltpu.VMEM
    dma = pltpu.SemaphoreType.DMA
    scratch = [
        V_((8, 2, 4, 2, 64, 1024), BF),
        V_((4, 1024, 512), BF),
        V_((4, 512, 1024), BF),
        V_((2, 256, 1024), BF),
        V_((2, 512, 1024), BF),
        V_((512, 1024), BF),
        V_((512, 1024), BF),
        V_((1024, 512), F32),
        V_((1024, 512), F32),
        V_((1024, 512), BF),
        V_((1024, 512), BF),
        V_((4, 1024, HD), BF),
        V_((4, 1024, HD), BF),
        V_((4, 1024), F32),
        V_((1024, HD), BF),
        V_((1024, HD), BF),
        V_((HD, 1024), BF),
        V_((4, 1024), F32),
        V_((4, 256, 1024), BF),
        V_((4, 256, 768), BF),
        V_((4, 256, 512), BF),
        V_((4, 256, 256), BF),
        V_((4, HD, 1024), F32),
        V_((4, 2, 2, 2, 32, 256), F32),
        V_((4, 2, 2, 2, 32, 256), BF),
        V_((4, 2, 2, 32, 256), F32),
        V_((4, 2, 2, 32, 256), BF),
        V_((4, 2, 2, 32, 256), BF),
        V_((4, 2, 32, 256), BF),
        dma, dma((8,)),
        dma, dma((4,)),
        dma, dma((8, 2)),
        dma, dma((8,)),
        dma, dma((8,)),
        dma, dma((6,)),
        dma, dma((6,)),
        dma, dma((4,)),
        dma, dma,
        dma((2,)), dma((2, 4)),
        dma((7,)),
    ]
    dq, dk, dv, wg = pl.pallas_call(
        kernel,
        out_shape=(
            V_((1024, 512), BF),
            V_((32, 1024), BF),
            V_((32, 1024), BF),
            V_((1024, 512), BF),
        ),
        in_specs=[any_spec] * 7,
        out_specs=(vmem,) * 4,
        scratch_shapes=scratch,
        compiler_params=pltpu.CompilerParams(
            collective_id=0, has_side_effects=True, vmem_limit_bytes=58_700_000
        ),
    )(grad_out, out_weight, query, keys, values, attended, stats)
    results = (dq, dk, dv, wg)
    dq, dk, dv, wg = pl.pallas_call(
        finish,
        out_shape=tuple(jax.ShapeDtypeStruct(r.shape, r.dtype) for r in results),
        in_specs=[any_spec] * 4,
        out_specs=(any_spec,) * 4,
        scratch_shapes=[dma((4,))],
        compiler_params=pltpu.CompilerParams(vmem_limit_bytes=1 << 20),
    )(*results)
    return (dq, dk.T, dv.T, wg)


def solution(mesh):
    torus = Mesh(mesh.devices.reshape(4, 2, 2, 4, 2), AXES)
    dp, tp = ("y", "xlo"), ("xhi", "z", "core")
    in_specs = (
        P(dp + tp, None),
        P(dp, tp),
        P(dp, tp),
        P(dp, None),
        P(dp, None),
        P(dp, tp),
        P(tp, dp),
    )
    out_specs = (P(dp, tp), P(dp, tp), P(dp, tp), P(dp, tp))
    return jax.shard_map(
        per_device, mesh=torus, in_specs=in_specs, out_specs=out_specs, check_vma=False
    )
```

time: 153 us -> 111 us (0.73)
  Pallas kernels: 146 us -> 108 us
  local copies, waits for them, and re-layouts: 4.86 us -> 0 us
    pallas_call x1 -> x2, Pallas kernels: 146 us -> 108 us  [the longest x1 107 us: per_device(): pl.pallas_call(kernel, out_shape=(V_((1024, 512), BF), V_((32, 1024), BF)...]
    unnamed x4 -> x0, local copies, waits for them, and re-layouts: 3.34 us -> none
where the time goes in v3:
time: 111 us; the launch traced here: 109 us
  Pallas kernels  108 us (97%)
    pallas_call x1, Pallas kernels, per_device(): pl.pallas_call(kernel, out_shape=(V_((1024, 512), BF), V_((32, 1024), BF)...  107 us

profile of v3, /device:TPU:1, one launch (start us, length us, event | category | flops | bytes accessed | tf_op | source)
XLA Modules:
  0.0 109.2 jit_solution(167461673204414324)
XLA Ops:
  0.6 107.0 %shard_map.102 = (bf16[1024,512]{1,0:T(8,128)(2,1)S(1)}, bf16[32,1024]{1,0:T(8,128)(2,1)S(1)}, bf16[32,1024]{1,0:T(8,128)(2,1)S(1)}, bf16[1024,512]{1,0:T(8,128)(2,1)S(1)}) custom-call(bf16[64,8192]{1,0:T(8,128)(2,1)} %g_in.1, bf16[1024,512]{1,0:T(8,128)(2,1)} %w_in.1, bf16[1024,512]{1,0:T(8,128)(2,1)} %q_in.1, bf16[1024,512]{1,0:T(8,128)(2,1)} %k_in.1, ...), custom_call_target="tpu_custom_call" | custom-call | tf_op jit(solution)/shard_map/pallas_call | solution.py:494
  107.7 1.4 %shard_map.103 = (bf16[1024,512]{1,0:T(8,128)(2,1)}, bf16[32,1024]{1,0:T(8,128)(2,1)}, bf16[32,1024]{1,0:T(8,128)(2,1)}, bf16[1024,512]{1,0:T(8,128)(2,1)}) custom-call(bf16[1024,512]{1,0:T(8,128)(2,1)S(1)} %get-tuple-element.12.refs_0_, bf16[32,1024]{1,0:T(8,128)(2,1)S(1)} %get-tuple-element.13.refs_1_, bf16[32,1024]{1,0:T(8,128)(2,1)S(1)} %get-tuple-element.14.refs_2_, ...), custom_call_target="tpu_custom_call" | custom-call | tf_op jit(solution)/shard_map/pallas_call | solution.py:510

commit v4 on v3

--- a/solution.py
+++ b/solution.py
@@ -49,16 +49,23 @@
     head = xhi * 2 + z // 2
     hcol = pl.ds(pl.multiple_of(head * HD, HD), HD)
     blocks = (y2, yp, ym, y)
-    own_chunk = (0, 5, 6, 7)
     pair_chunk = (1, 2, 3, 4)
 
-    def columns(q, x):
-        return pl.ds(pl.multiple_of((blocks[q] * 2 + x) * 1024, 1024), 1024)
-
-    for q in range(4):
+    def columns(q, x, first=0, count=1024):
+        return pl.ds(pl.multiple_of((blocks[q] * 2 + x) * 1024 + first, 512), count)
+
+    for q, j in ((0, 0), (3, 7)):
         pltpu.make_async_copy(
-            g_in.at[:, columns(q, xlo)], G.at[own_chunk[q], xhi, z, c], ls.at[0]
+            g_in.at[:, columns(q, xlo)], G.at[j, xhi, z, c], ls.at[0]
         ).start()
+    for q in (1, 2):
+        for half in range(2):
+            at = pl.ds((q - 1) * 512, 512)
+            pltpu.make_async_copy(
+                g_in.at[:, columns(q, xlo, half * 512, 512)],
+                G.at[5 + half, xhi, z, c, :, at],
+                ls.at[0],
+            ).start()
     wcp = pltpu.make_async_copy(w_in, W.at[0], ls.at[1])
     wcp.start()
     for h in range(4):
@@ -138,9 +145,10 @@
     rspec = (
         (S.at[0, up], RH.at[0], {"y": yp}),
         (S.at[0, dn], RH.at[1], {"y": ym}),
-        (S.at[1, dn], RY.at[0, dn], {"y": yp}),
-        (S.at[1, up], RY.at[0, up], {"y": yp}),
-        (S.at[2, up], RY.at[1, up], {"y": ym}),
+        (S.at[1, :, top], RY.at[0, :, top], {"y": yp}),
+        (S.at[1, :, low], RY.at[0, :, low], {"y": yp}),
+        (S.at[2, up, top], RY.at[1, up, top], {"y": ym}),
+        (S.at[2, up, low], RY.at[1, up, low], {"y": ym}),
         (S.at[2, dn], RY.at[1, dn], {"y": ym}),
     )
 
@@ -164,11 +172,12 @@
                 total = total + src[at].astype(F32)
             dst[at] = total.astype(BF)
 
-    def weight_part(q, rows):
-        @pl.loop(0, 4)
+    def weight_part(q, rows, j, shift=0, first=0, count=1024):
+        @pl.loop(0, count // 256)
         def _(n):
-            at = pl.ds(pl.multiple_of(n * 256, 256), 256)
-            mine = G[own_chunk[q], :, :, :, :, at].reshape(1024, 256)
+            at = pl.ds(pl.multiple_of(n * 256 + first, 256), 256)
+            own_at = pl.ds(pl.multiple_of(n * 256 + shift, 256), 256)
+            mine = G[j, :, :, :, :, own_at].reshape(1024, 256)
             pair = G[pair_chunk[q], :, :, :, :, at].reshape(1024, 256)
             S[q, rows, at] = (dot(AT[rows], mine) + dot(AT2[rows], pair)).astype(BF)
 
@@ -179,7 +188,10 @@
             def _(b):
                 at = pl.ds(pl.multiple_of((a * 2 + b) * 256, 256), 256)
                 rows = G[j, a, pl.ds(b * 2, 2)].reshape(256, 1024)
-                acc[at] += dot(rows, W[slot])
+                if isinstance(slot, int):
+                    acc[at] += dot(rows, W[slot])
+                else:
+                    acc[at] += dot(rows[:, :512], W[2, slot]) + dot(rows[:, 512:], W[1, slot])
 
     def w_start(*which):
         for n in which:
@@ -196,6 +208,8 @@
         u_send(0, d, 0).start()
     w_start(0, 1, 2, 3)
     x_send(0).start()
+    for d in range(2):
+        u_send(5, d, 0).start()
     e_send(0).start()
     e_send(1).start()
     pltpu.make_async_copy(GA, GA, ls.at[2]).wait()
@@ -219,137 +233,126 @@
             value = jnp.exp(scores - stat[:, lo:])
             PT[r][h] = jnp.where(keys_at <= query_at, value, 0.0).astype(BF)
 
-    def at_step(i, n, run):
-        @pl.when(i == n)
-        def _():
-            run()
-
-    @pl.loop(0, 11)
-    def _(i):
-        @pl.when(i < 8)
-        def _():
-            x_recv(i).wait_recv()
-            u_send(i, 0, 1).start()
-            u_send(i, 1, 1).start()
-            c_send(i, 0).start()
-
-        def feed(q):
-            e_recv(q).wait_recv()
-            x_send(q + 1).start()
-            for d in range(2):
-                u_send(q + 1, d, 0).start()
-
-        def feed_0():
-            feed(0)
-            e_send(2).start()
-
-        def feed_1():
-            feed(1)
-            e_send(3).start()
-            a_send(0).start()
-
-        def feed_2():
-            feed(2)
-            a_send(1).start()
-
-        def feed_3():
-            feed(3)
-            a_send(2).start()
-            x_send(5).start()
-
-        def feed_4():
-            a_send(3).start()
-            x_send(6).start()
-
-        def feed_5():
-            x_send(7).start()
-
-        for n, run in enumerate((feed_0, feed_1, feed_2, feed_3, feed_4, feed_5)):
-            at_step(i, n, run)
-
-        @pl.when(i >= 3)
-        def _():
-            c_recv(i - 3).wait_recv()
-
-        def pair_done():
-            att_part(PG, 4, 0)
-            PS[...] = PG[...].astype(BF)
-            p_send().start()
-
-        at_step(i, 7, pair_done)
-
-        @pl.when((i >= 1) & (i < 5))
-        def _():
-            prob_part(i - 1)
-
-        @pl.when((i >= 1) & (i < 9))
-        def _():
-            j = i - 1
-            for d in range(2):
-                u_recv(j, d).wait_recv()
-                z_send(j, d).start()
-            c_send(j, 1).start()
-            c_send(j, 2).start()
-
-        @pl.when((i >= 4) & (i < 7))
-        def _():
-            for d in range(2):
-                u_send(i + 1, d, 0).start()
-
-        def relay_w():
-            w_wait(0, 1)
-            w_start(4, 5)
-
-        at_step(i, 2, relay_w)
-
-        @pl.when((i >= 2) & (i < 10))
-        def _():
-            j = i - 2
-            z_recv(j).wait_recv()
-            c_send(j, 3).start()
-
-        def step_4():
-            w_wait(2, 3, 4, 5)
-            att_part(ACC, 0, 3)
-
-        def step_5():
-            a_send(0).wait_recv()
-            a_send(1).wait_recv()
-            weight_part(0, up)
-            r_send(0).start()
-            att_part(PG, 1, 3)
-            att_part(PG, 2, 2)
-
-        def step_6():
-            att_part(PG, 3, 1)
-            a_send(2).wait_recv()
-            a_send(3).wait_recv()
-            weight_part(0, dn)
-            r_send(1).start()
-
-        def step_8():
-            weight_part(1, pl.ds(0, 512))
-            r_send(2).start()
-            r_send(0).wait_recv()
-            add_into(S.at[1, up], 256, [RH.at[0]])
-            r_send(3).start()
-            att_part(ACC, 5, 2)
-
-        def step_9():
-            weight_part(2, pl.ds(0, 512))
-            r_send(4).start()
-            r_send(1).wait_recv()
-            add_into(S.at[2, dn], 256, [RH.at[1]])
-            r_send(5).start()
-            att_part(ACC, 6, 1)
-
-        def step_10():
-            att_part(ACC, 7, 0)
-            weight_part(3, pl.ds(0, 512))
-
-        for n, run in ((4, step_4), (5, step_5), (6, step_6), (8, step_8), (9, step_9), (10, step_10)):
-            at_step(i, n, run)
-
+    every = pl.ds(0, 512)
+
+    def u_own(j):
+        for d in range(2):
+            u_send(j, d, 0).start()
+
+    def pump(j):
+        x_recv(j).wait_recv()
+        u_send(j, 0, 1).start()
+        u_send(j, 1, 1).start()
+        c_send(j, 0).start()
+
+    def feed(q):
+        e_recv(q).wait_recv()
+        x_send(q + 1).start()
+        u_own(q + 1)
+
+    def relay(j):
+        for d in range(2):
+            u_recv(j, d).wait_recv()
+            z_send(j, d).start()
+        c_send(j, 1).start()
+        c_send(j, 2).start()
+
+    def land(j):
+        z_recv(j).wait_recv()
+        c_send(j, 3).start()
+
+    def take(j):
+        c_recv(j).wait_recv()
+
+    def a_wait(*which):
+        for h in which:
+            a_send(h).wait_recv()
+
+    pump(0)
+    feed(0)
+    e_send(2).start()
+    feed(1)
+    e_send(3).start()
+    prob_part(0)
+    relay(0)
+    pump(1)
+    feed(2)
+    w_wait(0, 1)
+    w_start(4, 5)
+    prob_part(1)
+    pump(2)
+    feed(3)
+    a_send(0).start()
+    a_send(1).start()
+    x_send(5).start()
+    a_send(2).start()
+    x_send(6).start()
+    a_send(3).start()
+    x_send(7).start()
+    relay(1)
+    land(0)
+    prob_part(2)
+    pump(3)
+    prob_part(3)
+    relay(2)
+    pump(4)
+    land(1)
+    take(0)
+    w_wait(2, 3, 4, 5)
+    att_part(ACC, 0, 3)
+    relay(3)
+    take(1)
+    att_part(PG, 1, 3)
+    land(2)
+    a_wait(0, 1)
+    weight_part(0, up, 0)
+    r_send(0).start()
+    relay(4)
+    u_own(6)
+    pump(5)
+    u_own(7)
+    take(2)
+    att_part(PG, 2, 2)
+    land(3)
+    take(3)
+    att_part(PG, 3, 1)
+    land(4)
+    pump(6)
+    take(4)
+    att_part(PG, 4, 0)
+    PS[...] = PG[...].astype(BF)
+    p_send().start()
+    relay(5)
+    a_wait(2, 3)
+    weight_part(0, dn, 0)
+    r_send(1).start()
+    pump(7)
+    land(5)
+    relay(6)
+    take(5)
+    weight_part(1, every, 5, 0, 0, 512)
+    r_send(0).wait_recv()
+    add_into(S.at[1, up, top], 256, [RH.at[0, :, top]])
+    r_send(2).start()
+    weight_part(2, every, 5, 512, 0, 512)
+    r_send(4).start()
+    relay(7)
+    land(6)
+    att_part(ACC, 5, top)
+    take(6)
+    weight_part(1, every, 6, 0, 512, 512)
+    add_into(S.at[1, up, low], 256, [RH.at[0, :, low]])
+    r_send(3).start()
+    weight_part(2, every, 6, 512, 512, 512)
+    r_send(5).start()
+    land(7)
+    r_send(1).wait_recv()
+    add_into(S.at[2, dn], 256, [RH.at[1]])
+    r_send(6).start()
+    att_part(ACC, 6, low)
+    take(7)
+    att_part(ACC, 7, 0)
+    weight_part(3, every, 7)
     p_send().wait_recv()
     for h in range(4):
         cols = slice(h * HD, (h + 1) * HD)
@@ -415,8 +418,11 @@
         ACC[:, at] = (S[3, at].astype(F32) + RY[0, at].astype(F32)).T
     for n in range(4):
         at = slice(n * HD, (n + 1) * HD)
-        if n % 2 == 0:
-            r_send(4 + n // 2).wait_recv()
+        if n == 0:
+            r_send(4).wait_recv()
+            r_send(5).wait_recv()
+        if n == 2:
+            r_send(6).wait_recv()
         wg_out[:, at] = (ACC[:, at] + RY[1, at].T.astype(F32)).astype(BF)
 
     for ref, sem in (
@@ -485,7 +491,7 @@
         dma, dma((8,)),
         dma, dma((8,)),
         dma, dma((6,)),
-        dma, dma((6,)),
+        dma, dma((7,)),
         dma, dma((4,)),
         dma, dma,
         dma((2,)), dma((2, 4)),

time: 111 us -> 101 us (0.910); the launches traced: 109 us -> 101 us
  Pallas kernels: 108 us -> 100 us
    pallas_call x1, Pallas kernels: 107 us -> 98.8 us  [per_device(): pl.pallas_call(kernel, out_shape=(V_((1024, 512), BF), V_((32, 1024), BF)...]
where the time goes in v4:
time: 101 us
  Pallas kernels  100 us (99%)
    pallas_call x1, Pallas kernels, per_device(): pl.pallas_call(kernel, out_shape=(V_((1024, 512), BF), V_((32, 1024), BF)...  98.8 us

profile of v4, /device:TPU:1, one launch (start us, length us, event | category | flops | bytes accessed | tf_op | source)
XLA Modules:
  0.0 101.0 jit_solution(10776963352681689663)
XLA Ops:
  0.6 98.8 %shard_map.102 = (bf16[1024,512]{1,0:T(8,128)(2,1)S(1)}, bf16[32,1024]{1,0:T(8,128)(2,1)S(1)}, bf16[32,1024]{1,0:T(8,128)(2,1)S(1)}, bf16[1024,512]{1,0:T(8,128)(2,1)S(1)}) custom-call(bf16[64,8192]{1,0:T(8,128)(2,1)} %g_in.1, bf16[1024,512]{1,0:T(8,128)(2,1)} %w_in.1, bf16[1024,512]{1,0:T(8,128)(2,1)} %q_in.1, bf16[1024,512]{1,0:T(8,128)(2,1)} %k_in.1, ...), custom_call_target="tpu_custom_call" | custom-call | tf_op jit(solution)/shard_map/pallas_call | solution.py:500
  99.5 1.4 %shard_map.103 = (bf16[1024,512]{1,0:T(8,128)(2,1)}, bf16[32,1024]{1,0:T(8,128)(2,1)}, bf16[32,1024]{1,0:T(8,128)(2,1)}, bf16[1024,512]{1,0:T(8,128)(2,1)}) custom-call(bf16[1024,512]{1,0:T(8,128)(2,1)S(1)} %get-tuple-element.12.refs_0_, bf16[32,1024]{1,0:T(8,128)(2,1)S(1)} %get-tuple-element.13.refs_1_, bf16[32,1024]{1,0:T(8,128)(2,1)S(1)} %get-tuple-element.14.refs_2_, ...), custom_call_target="tpu_custom_call" | custom-call | tf_op jit(solution)/shard_map/pallas_call | solution.py:516

commit v5 on v4

--- a/solution.py
+++ b/solution.py
@@ -33,8 +33,8 @@
 def kernel(
     g_in, w_in, q_in, k_in, v_in, a_in, st_in,
     dq_out, dk_out, dv_out, wg_out,
-    G, W, S, RH, RY, AT, AT2, ACC, PG, PS, PR, Q, GA, OFF, K, V, KT, ST,
-    P0, P1, P2, P3, DQ, KF, KB, KS, KR1, KB2, KR2,
+    G, W, S, RH, RY, AT, AT2, WT, ACC, PG, PS, PR, Q, GA, K, V, KT, ST,
+    P0, P1, P2, P3, DQ, DK, DV, KF, KB, KS, KR1, KB2, KR2,
     xs, xr, es, er, us, ur, zs, zr, cs, cr, ws, wr, rs, rr, ats, atr, ps, pr, ks, kr, ls,
 ):
     y, xlo, xhi = lax.axis_index("y"), lax.axis_index("xlo"), lax.axis_index("xhi")
@@ -80,17 +80,21 @@
         cp.start()
 
     barrier = pltpu.get_barrier_semaphore()
-    for dev in ({"y": yp}, {"y": ym}, {"xlo": xo}, {"xhi": xh}, {"z": zp}, {"z": zm}, {"core": co}):
+    for dev in (
+        {"y": yp}, {"y": ym}, {"z": zp}, {"z": zm}, {"core": co},
+        {"xlo": xo}, {"xhi": xh}, {"xlo": xo, "xhi": xh},
+    ):
         pl.semaphore_signal(barrier, inc=1, device_id=dev, device_id_type=pl.DeviceIdType.MESH)
-    pl.semaphore_wait(barrier, 7)
-
-    def e_send(q):
+    pl.semaphore_wait(barrier, 8)
+
+    def e_send(q, other):
         dst = G.at[pair_chunk[q], xhi, z, c]
-        return rcopy(g_in.at[:, columns(q, xo)], dst, es, er.at[q], {"xlo": xo})
-
-    def e_recv(q):
-        dst = G.at[pair_chunk[q], xhi, z, c]
-        return rcopy(dst, dst, es, er.at[q], {"xlo": xo})
+        dev = {"xlo": xo, "xhi": xh} if other else {"xlo": xo}
+        return rcopy(g_in.at[:, columns(q, xo)], dst, es, er.at[q, other], dev)
+
+    def e_recv(q, other):
+        dst = G.at[pair_chunk[q], (xhi, xh)[other], z, c]
+        return rcopy(dst, dst, es, er.at[q, other], {"xlo": xo})
 
     def x_send(j):
         return rcopy(G.at[j, xhi, z, c], G.at[j, xhi, z, c], xs, xr.at[j], {"xhi": xh})
@@ -147,9 +151,8 @@
         (S.at[0, dn], RH.at[1], {"y": ym}),
         (S.at[1, :, top], RY.at[0, :, top], {"y": yp}),
         (S.at[1, :, low], RY.at[0, :, low], {"y": yp}),
-        (S.at[2, up, top], RY.at[1, up, top], {"y": ym}),
-        (S.at[2, up, low], RY.at[1, up, low], {"y": ym}),
-        (S.at[2, dn], RY.at[1, dn], {"y": ym}),
+        (S.at[2, :, top], RY.at[1, :, top], {"y": ym}),
+        (S.at[2, :, low], RY.at[1, :, low], {"y": ym}),
     )
 
     def r_send(n):
@@ -160,8 +163,8 @@
         at = pl.ds(h * HD, HD)
         return rcopy(AT.at[at], AT2.at[at], ats, atr.at[h], {"xlo": xo})
 
-    def p_send():
-        return rcopy(PS, PR, ps, pr, {"xlo": xo})
+    def p_send(h):
+        return rcopy(PS.at[h], PR.at[h], ps, pr.at[h], {"xlo": xo})
 
     def add_into(dst, rows, srcs):
         @pl.loop(0, rows // 64)
@@ -172,26 +175,41 @@
                 total = total + src[at].astype(F32)
             dst[at] = total.astype(BF)
 
-    def weight_part(q, rows, j, shift=0, first=0, count=1024):
+    def columns_of(j, at):
+        return G[j, :, :, :, :, at].reshape(1024, 256)
+
+    def tile(n, first=0):
+        return pl.ds(pl.multiple_of(n * 256 + first, 256), 256)
+
+    def weight_part(rows):
+        @pl.loop(0, 4)
+        def _(n):
+            at = tile(n)
+            total = dot(AT[rows], columns_of(0, at)) + dot(AT2[rows], columns_of(1, at))
+            S[0, rows, at] = total.astype(BF)
+
+    def pair_part(q):
+        @pl.loop(0, 4)
+        def _(n):
+            at = tile(n)
+            WT[q - 1, :, at] = dot(AT2[...], columns_of(pair_chunk[q], at))
+
+    def own_part(q, j, shift, first, count):
         @pl.loop(0, count // 256)
         def _(n):
-            at = pl.ds(pl.multiple_of(n * 256 + first, 256), 256)
-            own_at = pl.ds(pl.multiple_of(n * 256 + shift, 256), 256)
-            mine = G[j, :, :, :, :, own_at].reshape(1024, 256)
-            pair = G[pair_chunk[q], :, :, :, :, at].reshape(1024, 256)
-            S[q, rows, at] = (dot(AT[rows], mine) + dot(AT2[rows], pair)).astype(BF)
+            at = tile(n, first)
+            total = WT[q - 1, :, at] + dot(AT[...], columns_of(j, tile(n, shift)))
+            S[q, :, at] = total.astype(BF)
 
     def att_part(acc, j, slot):
         @pl.loop(0, 2)
         def _(a):
-            @pl.loop(0, 2)
-            def _(b):
-                at = pl.ds(pl.multiple_of((a * 2 + b) * 256, 256), 256)
-                rows = G[j, a, pl.ds(b * 2, 2)].reshape(256, 1024)
-                if isinstance(slot, int):
-                    acc[at] += dot(rows, W[slot])
-                else:
-                    acc[at] += dot(rows[:, :512], W[2, slot]) + dot(rows[:, 512:], W[1, slot])
+            at = pl.ds(pl.multiple_of(a * 512, 512), 512)
+            rows = G[j, a].reshape(512, 1024)
+            if isinstance(slot, int):
+                acc[at] += dot(rows, W[slot])
+            else:
+                acc[at] += dot(rows[:, :512], W[2, slot]) + dot(rows[:, 512:], W[1, slot])
 
     def w_start(*which):
         for n in which:
@@ -210,8 +228,9 @@
     x_send(0).start()
     for d in range(2):
         u_send(5, d, 0).start()
-    e_send(0).start()
-    e_send(1).start()
+    for q in range(4):
+        for other in range(2):
+            e_send(q, other).start()
     pltpu.make_async_copy(GA, GA, ls.at[2]).wait()
     for h in range(4):
         AT[h * HD : (h + 1) * HD] = GA[h].T
@@ -233,21 +252,21 @@
             value = jnp.exp(scores - stat[:, lo:])
             PT[r][h] = jnp.where(keys_at <= query_at, value, 0.0).astype(BF)
 
-    every = pl.ds(0, 512)
-
     def u_own(j):
         for d in range(2):
             u_send(j, d, 0).start()
 
     def pump(j):
-        x_recv(j).wait_recv()
+        if j in pair_chunk:
+            e_recv(j - 1, 1).wait_recv()
+        else:
+            x_recv(j).wait_recv()
         u_send(j, 0, 1).start()
         u_send(j, 1, 1).start()
         c_send(j, 0).start()
 
     def feed(q):
-        e_recv(q).wait_recv()
-        x_send(q + 1).start()
+        e_recv(q, 0).wait_recv()
         u_own(q + 1)
 
     def relay(j):
@@ -268,98 +287,89 @@
         for h in which:
             a_send(h).wait_recv()
 
+    for h in range(4):
+        a_send(h).start()
+    for j in (5, 6, 7):
+        x_send(j).start()
     pump(0)
     feed(0)
-    e_send(2).start()
-    feed(1)
-    e_send(3).start()
+    pump(1)
     prob_part(0)
     relay(0)
-    pump(1)
-    feed(2)
+    feed(1)
+    pump(2)
     w_wait(0, 1)
     w_start(4, 5)
     prob_part(1)
-    pump(2)
-    feed(3)
-    a_send(0).start()
-    a_send(1).start()
-    x_send(5).start()
-    a_send(2).start()
-    x_send(6).start()
-    a_send(3).start()
-    x_send(7).start()
     relay(1)
+    feed(2)
+    pump(3)
+    prob_part(2)
     land(0)
-    prob_part(2)
-    pump(3)
     prob_part(3)
     relay(2)
+    feed(3)
     pump(4)
     land(1)
     take(0)
+    take(1)
+    a_wait(0, 1)
+    weight_part(up)
+    r_send(0).start()
+    relay(3)
     w_wait(2, 3, 4, 5)
     att_part(ACC, 0, 3)
-    relay(3)
-    take(1)
+    land(2)
     att_part(PG, 1, 3)
-    land(2)
-    a_wait(0, 1)
-    weight_part(0, up, 0)
-    r_send(0).start()
+    take(2)
+    a_wait(2, 3)
+    weight_part(dn)
+    r_send(1).start()
     relay(4)
+    pump(5)
     u_own(6)
-    pump(5)
-    u_own(7)
-    take(2)
     att_part(PG, 2, 2)
     land(3)
     take(3)
     att_part(PG, 3, 1)
     land(4)
+    relay(5)
     pump(6)
+    u_own(7)
+    pump(7)
     take(4)
     att_part(PG, 4, 0)
-    PS[...] = PG[...].astype(BF)
-    p_send().start()
-    relay(5)
-    a_wait(2, 3)
-    weight_part(0, dn, 0)
-    r_send(1).start()
-    pump(7)
+    for h in range(4):
+        PS[h] = PG[:, h * HD : (h + 1) * HD].astype(BF)
+        p_send(h).start()
+    pair_part(1)
     land(5)
-    relay(6)
+    pair_part(2)
     take(5)
-    weight_part(1, every, 5, 0, 0, 512)
+    own_part(1, 5, 0, 0, 512)
     r_send(0).wait_recv()
     add_into(S.at[1, up, top], 256, [RH.at[0, :, top]])
     r_send(2).start()
-    weight_part(2, every, 5, 512, 0, 512)
+    relay(6)
+    own_part(2, 5, 512, 0, 512)
+    r_send(1).wait_recv()
+    add_into(S.at[2, dn, top], 256, [RH.at[1, :, top]])
     r_send(4).start()
+    pair_part(3)
+    att_part(ACC, 5, top)
     relay(7)
     land(6)
-    att_part(ACC, 5, top)
     take(6)
-    weight_part(1, every, 6, 0, 512, 512)
+    own_part(1, 6, 0, 512, 512)
     add_into(S.at[1, up, low], 256, [RH.at[0, :, low]])
     r_send(3).start()
-    weight_part(2, every, 6, 512, 512, 512)
+    own_part(2, 6, 512, 512, 512)
+    add_into(S.at[2, dn, low], 256, [RH.at[1, :, low]])
     r_send(5).start()
     land(7)
-    r_send(1).wait_recv()
-    add_into(S.at[2, dn], 256, [RH.at[1]])
-    r_send(6).start()
     att_part(ACC, 6, low)
     take(7)
     att_part(ACC, 7, 0)
-    weight_part(3, every, 7)
-    p_send().wait_recv()
-    for h in range(4):
-        cols = slice(h * HD, (h + 1) * HD)
-        part = (ACC[:, cols] + PR[:, cols].astype(F32)).astype(BF)
-        GA[h] = part
-        both = part.T.astype(F32) * AT[h * HD : (h + 1) * HD].astype(F32)
-        OFF[h : h + 1] = jnp.sum(both, axis=0, keepdims=True)
 
     zh = lax.rem(z, 2)
 
@@ -378,61 +388,68 @@
                 KB2[r, half, n] = total.astype(BF)
         kv_second(r).start()
 
-    for r in range(4):
-        lo = r * 256
-        mine = slice(lo, lo + 256)
-        dv = jnp.zeros((256, HD), F32)
-        dk = jnp.zeros((256, HD), F32)
-        for h in range(4):
+    for h in range(4):
+        cols = slice(h * HD, (h + 1) * HD)
+        p_send(h).wait_recv()
+        part = (ACC[:, cols] + PR[h].astype(F32)).astype(BF)
+        GA[h] = part
+        offset = jnp.sum(part.T.astype(F32) * AT[cols].astype(F32), axis=0, keepdims=True)
+        for r in range(4):
+            lo = r * 256
+            mine = slice(lo, lo + 256)
             attention = PT[r][h]
             gb = GA[h, lo:]
-            dv = dv + dot(attention, gb)
+            dv = dot(attention, gb)
             grad_att = dot(V[mine], gb, NT)
-            grad_scores = (attention.astype(F32) * (grad_att - OFF[h : h + 1, lo:])).astype(BF)
-            dk = dk + dot(grad_scores, Q[h, lo:])
+            grad_scores = (attention.astype(F32) * (grad_att - offset[:, lo:])).astype(BF)
+            dk = dot(grad_scores, Q[h, lo:])
             dq = dot(KT[:, mine], grad_scores)
             if r > 0:
-                dq = dq + DQ[h, :, lo:]
-            DQ[h, :, lo:] = dq
-            dq_out[mine, h * HD : (h + 1) * HD] = (dq[:, :256] * scale).T.astype(BF)
-        for n, full in enumerate(((dk * scale).T, dv.T)):
-            for half in range(2):
-                for core in range(2):
-                    at = half * 64 + core * 32
-                    KF[r, n, half, core] = full[at : at + 32]
-                    KB[r, n, half, core] = full[at : at + 32].astype(BF)
-        kv_first(r).start()
-        if r > 0:
-            kv_middle(r - 1)
+                dq = dq + DQ[:, lo:]
+            DQ[:, lo:] = dq
+            dq_out[mine, cols] = (dq[:, :256] * scale).T.astype(BF)
+            if h > 0:
+                dv = dv + DV[r]
+                dk = dk + DK[r]
+            if h < 3:
+                DV[r] = dv
+                DK[r] = dk
+                continue
+            for n, full in enumerate(((dk * scale).T, dv.T)):
+                for half in range(2):
+                    for core in range(2):
+                        at = half * 64 + core * 32
+                        KF[r, n, half, core] = full[at : at + 32]
+                        KB[r, n, half, core] = full[at : at + 32].astype(BF)
+            kv_first(r).start()
+            if r > 0:
+                kv_middle(r - 1)
     kv_middle(3)
+    for half in range(2):
+        r_send(2 + half).wait_recv()
+        r_send(4 + half).wait_recv()
+
+        @pl.loop(0, 2)
+        def _(n):
+            at = tile(n, half * 512)
+            total = WT[2, :, at] + dot(AT[...], columns_of(7, at))
+            total = total + RY[0, :, at].astype(F32) + RY[1, :, at].astype(F32)
+            wg_out[at] = total.T.astype(BF)
+
     for r in range(4):
         kv_second(r).wait_recv()
         for n in range(2):
             total = KS[r, n, zh] + KR2[r, n].astype(F32)
             (dk_out, dv_out)[n][:, r * 256 : r * 256 + 256] = total.astype(BF)
 
-    r_send(2).wait_recv()
-    r_send(3).wait_recv()
-    for n in range(4):
-        at = slice(n * HD, (n + 1) * HD)
-        ACC[:, at] = (S[3, at].astype(F32) + RY[0, at].astype(F32)).T
-    for n in range(4):
-        at = slice(n * HD, (n + 1) * HD)
-        if n == 0:
-            r_send(4).wait_recv()
-            r_send(5).wait_recv()
-        if n == 2:
-            r_send(6).wait_recv()
-        wg_out[:, at] = (ACC[:, at] + RY[1, at].T.astype(F32)).astype(BF)
-
     for ref, sem in (
-        (first, es),
-        (G.at[:, 0, 0, 0], xs),
+        (G.at[:, 0, 0, 0], es),
+        (first, xs),
         (G.at[pl.ds(0, 2)], us),
         (G.at[0], zs),
         (G.at[pl.ds(0, 4)], cs),
         (W.at[pl.ds(0, 3)], ws),
-        (S.at[pl.ds(0, 3)], rs),
+        (S, rs),
         (AT, ats),
         (PS, ps),
         (KR1, ks.at[0]),
@@ -458,18 +475,18 @@
     scratch = [
         V_((8, 2, 4, 2, 64, 1024), BF),
         V_((4, 1024, 512), BF),
-        V_((4, 512, 1024), BF),
+        V_((3, 512, 1024), BF),
         V_((2, 256, 1024), BF),
         V_((2, 512, 1024), BF),
         V_((512, 1024), BF),
         V_((512, 1024), BF),
+        V_((3, 512, 1024), F32),
         V_((1024, 512), F32),
         V_((1024, 512), F32),
-        V_((1024, 512), BF),
-        V_((1024, 512), BF),
         V_((4, 1024, HD), BF),
         V_((4, 1024, HD), BF),
-        V_((4, 1024), F32),
+        V_((4, 1024, HD), BF),
+        V_((4, 1024, HD), BF),
         V_((1024, HD), BF),
         V_((1024, HD), BF),
         V_((HD, 1024), BF),
@@ -478,7 +495,9 @@
         V_((4, 256, 768), BF),
         V_((4, 256, 512), BF),
         V_((4, 256, 256), BF),
-        V_((4, HD, 1024), F32),
+        V_((HD, 1024), F32),
+        V_((4, 256, HD), F32),
+        V_((4, 256, HD), F32),
         V_((4, 2, 2, 2, 32, 256), F32),
         V_((4, 2, 2, 2, 32, 256), BF),
         V_((4, 2, 2, 32, 256), F32),
@@ -486,14 +505,14 @@
         V_((4, 2, 2, 32, 256), BF),
         V_((4, 2, 32, 256), BF),
         dma, dma((8,)),
-        dma, dma((4,)),
+        dma, dma((4, 2)),
         dma, dma((8, 2)),
         dma, dma((8,)),
         dma, dma((8,)),
         dma, dma((6,)),
-        dma, dma((7,)),
+        dma, dma((6,)),
         dma, dma((4,)),
-        dma, dma,
+        dma, dma((4,)),
         dma((2,)), dma((2, 4)),
         dma((7,)),
     ]

time: 101 us -> 96.8 us (0.958)
  Pallas kernels: 100 us -> 95.8 us
    pallas_call x1, Pallas kernels: 98.8 us -> 94.4 us  [per_device(): pl.pallas_call(kernel, out_shape=(V_((1024, 512), BF), V_((32, 1024), BF)...]
where the time goes in v5:
time: 96.8 us; the launch traced here: 96.6 us
  Pallas kernels  95.8 us (99%)
    pallas_call x1, Pallas kernels, per_device(): pl.pallas_call(kernel, out_shape=(V_((1024, 512), BF), V_((32, 1024), BF)...  94.4 us

profile of v5, /device:TPU:1, one launch (start us, length us, event | category | flops | bytes accessed | tf_op | source)
XLA Modules:
  0.0 96.6 jit_solution(3631109173293387147)
XLA Ops:
  0.6 94.4 %shard_map.102 = (bf16[1024,512]{1,0:T(8,128)(2,1)S(1)}, bf16[32,1024]{1,0:T(8,128)(2,1)S(1)}, bf16[32,1024]{1,0:T(8,128)(2,1)S(1)}, bf16[1024,512]{1,0:T(8,128)(2,1)S(1)}) custom-call(bf16[64,8192]{1,0:T(8,128)(2,1)} %g_in.1, bf16[1024,512]{1,0:T(8,128)(2,1)} %w_in.1, bf16[1024,512]{1,0:T(8,128)(2,1)} %q_in.1, bf16[1024,512]{1,0:T(8,128)(2,1)} %k_in.1, ...), custom_call_target="tpu_custom_call" | custom-call | tf_op jit(solution)/shard_map/pallas_call | solution.py:519
  95.1 1.4 %shard_map.103 = (bf16[1024,512]{1,0:T(8,128)(2,1)}, bf16[32,1024]{1,0:T(8,128)(2,1)}, bf16[32,1024]{1,0:T(8,128)(2,1)}, bf16[1024,512]{1,0:T(8,128)(2,1)}) custom-call(bf16[1024,512]{1,0:T(8,128)(2,1)S(1)} %get-tuple-element.12.refs_0_, bf16[32,1024]{1,0:T(8,128)(2,1)S(1)} %get-tuple-element.13.refs_1_, bf16[32,1024]{1,0:T(8,128)(2,1)S(1)} %get-tuple-element.14.refs_2_, ...), custom_call_target="tpu_custom_call" | custom-call | tf_op jit(solution)/shard_map/pallas_call | solution.py:535

commit v6 on v5

--- a/solution.py
+++ b/solution.py
@@ -176,26 +176,26 @@
             dst[at] = total.astype(BF)
 
     def columns_of(j, at):
-        return G[j, :, :, :, :, at].reshape(1024, 256)
+        return G[j, :, :, :, :, at].reshape(1024, 512)
 
     def tile(n, first=0):
-        return pl.ds(pl.multiple_of(n * 256 + first, 256), 256)
+        return pl.ds(pl.multiple_of(n * 512 + first, 512), 512)
 
     def weight_part(rows):
-        @pl.loop(0, 4)
+        @pl.loop(0, 2)
         def _(n):
             at = tile(n)
             total = dot(AT[rows], columns_of(0, at)) + dot(AT2[rows], columns_of(1, at))
             S[0, rows, at] = total.astype(BF)
 
     def pair_part(q):
-        @pl.loop(0, 4)
+        @pl.loop(0, 2)
         def _(n):
             at = tile(n)
             WT[q - 1, :, at] = dot(AT2[...], columns_of(pair_chunk[q], at))
 
     def own_part(q, j, shift, first, count):
-        @pl.loop(0, count // 256)
+        @pl.loop(0, count // 512)
         def _(n):
             at = tile(n, first)
             total = WT[q - 1, :, at] + dot(AT[...], columns_of(j, tile(n, shift)))
@@ -350,11 +350,11 @@
     r_send(0).wait_recv()
     add_into(S.at[1, up, top], 256, [RH.at[0, :, top]])
     r_send(2).start()
-    relay(6)
     own_part(2, 5, 512, 0, 512)
     r_send(1).wait_recv()
     add_into(S.at[2, dn, top], 256, [RH.at[1, :, top]])
     r_send(4).start()
+    relay(6)
     pair_part(3)
     att_part(ACC, 5, top)
     relay(7)
@@ -429,12 +429,10 @@
         r_send(2 + half).wait_recv()
         r_send(4 + half).wait_recv()
 
-        @pl.loop(0, 2)
-        def _(n):
-            at = tile(n, half * 512)
-            total = WT[2, :, at] + dot(AT[...], columns_of(7, at))
-            total = total + RY[0, :, at].astype(F32) + RY[1, :, at].astype(F32)
-            wg_out[at] = total.T.astype(BF)
+        at = tile(half)
+        total = WT[2, :, at] + dot(AT[...], columns_of(7, at))
+        total = total + RY[0, :, at].astype(F32) + RY[1, :, at].astype(F32)
+        wg_out[at] = total.T.astype(BF)
 
     for r in range(4):
         kv_second(r).wait_recv()

time: 96.8 us -> 96 us (level)
  no operation moved by 1% of the time
where the time goes in v6:
time: 96 us; the launch traced here: 95.9 us
  Pallas kernels  95.1 us (99%)
    pallas_call x1, Pallas kernels, per_device(): pl.pallas_call(kernel, out_shape=(V_((1024, 512), BF), V_((32, 1024), BF)...  93.7 us

profile of v6, /device:TPU:1, one launch (start us, length us, event | category | flops | bytes accessed | tf_op | source)
XLA Modules:
  0.0 95.9 jit_solution(4649951756287293768)
XLA Ops:
  0.6 93.7 %shard_map.102 = (bf16[1024,512]{1,0:T(8,128)(2,1)S(1)}, bf16[32,1024]{1,0:T(8,128)(2,1)S(1)}, bf16[32,1024]{1,0:T(8,128)(2,1)S(1)}, bf16[1024,512]{1,0:T(8,128)(2,1)S(1)}) custom-call(bf16[64,8192]{1,0:T(8,128)(2,1)} %g_in.1, bf16[1024,512]{1,0:T(8,128)(2,1)} %w_in.1, bf16[1024,512]{1,0:T(8,128)(2,1)} %q_in.1, bf16[1024,512]{1,0:T(8,128)(2,1)} %k_in.1, ...), custom_call_target="tpu_custom_call" | custom-call | tf_op jit(solution)/shard_map/pallas_call | solution.py:517
  94.3 1.4 %shard_map.103 = (bf16[1024,512]{1,0:T(8,128)(2,1)}, bf16[32,1024]{1,0:T(8,128)(2,1)}, bf16[32,1024]{1,0:T(8,128)(2,1)}, bf16[1024,512]{1,0:T(8,128)(2,1)}) custom-call(bf16[1024,512]{1,0:T(8,128)(2,1)S(1)} %get-tuple-element.12.refs_0_, bf16[32,1024]{1,0:T(8,128)(2,1)S(1)} %get-tuple-element.13.refs_1_, bf16[32,1024]{1,0:T(8,128)(2,1)S(1)} %get-tuple-element.14.refs_2_, ...), custom_call_target="tpu_custom_call" | custom-call | tf_op jit(solution)/shard_map/pallas_call | solution.py:533

commit v7 on v6

--- a/solution.py
+++ b/solution.py
@@ -426,12 +426,13 @@
                 kv_middle(r - 1)
     kv_middle(3)
     for half in range(2):
+        at = tile(half)
+        WT[2, :, at] += dot(AT[...], columns_of(7, at))
+    for half in range(2):
         r_send(2 + half).wait_recv()
         r_send(4 + half).wait_recv()
-
         at = tile(half)
-        total = WT[2, :, at] + dot(AT[...], columns_of(7, at))
-        total = total + RY[0, :, at].astype(F32) + RY[1, :, at].astype(F32)
+        total = WT[2, :, at] + RY[0, :, at].astype(F32) + RY[1, :, at].astype(F32)
         wg_out[at] = total.T.astype(BF)
 
     for r in range(4):

time: 96 us -> 95.5 us (level)
  no operation moved by 1% of the time
where the time goes in v7:
time: 95.5 us; the launch traced here: 95.4 us
  Pallas kernels  94.6 us (99%)
    pallas_call x1, Pallas kernels, per_device(): pl.pallas_call(kernel, out_shape=(V_((1024, 512), BF), V_((32, 1024), BF)...  93.2 us

profile of v7, /device:TPU:1, one launch (start us, length us, event | category | flops | bytes accessed | tf_op | source)
XLA Modules:
  0.0 95.4 jit_solution(2616987928545820024)
XLA Ops:
  0.6 93.2 %shard_map.102 = (bf16[1024,512]{1,0:T(8,128)(2,1)S(1)}, bf16[32,1024]{1,0:T(8,128)(2,1)S(1)}, bf16[32,1024]{1,0:T(8,128)(2,1)S(1)}, bf16[1024,512]{1,0:T(8,128)(2,1)S(1)}) custom-call(bf16[64,8192]{1,0:T(8,128)(2,1)} %g_in.1, bf16[1024,512]{1,0:T(8,128)(2,1)} %w_in.1, bf16[1024,512]{1,0:T(8,128)(2,1)} %q_in.1, bf16[1024,512]{1,0:T(8,128)(2,1)} %k_in.1, ...), custom_call_target="tpu_custom_call" | custom-call | tf_op jit(solution)/shard_map/pallas_call | solution.py:518
  93.9 1.4 %shard_map.103 = (bf16[1024,512]{1,0:T(8,128)(2,1)}, bf16[32,1024]{1,0:T(8,128)(2,1)}, bf16[32,1024]{1,0:T(8,128)(2,1)}, bf16[1024,512]{1,0:T(8,128)(2,1)}) custom-call(bf16[1024,512]{1,0:T(8,128)(2,1)S(1)} %get-tuple-element.12.refs_0_, bf16[32,1024]{1,0:T(8,128)(2,1)S(1)} %get-tuple-element.13.refs_1_, bf16[32,1024]{1,0:T(8,128)(2,1)S(1)} %get-tuple-element.14.refs_2_, ...), custom_call_target="tpu_custom_call" | custom-call | tf_op jit(solution)/shard_map/pallas_call | solution.py:534
